TPU v7x, 16 devices: a 4x2x1 block of a 4x4x8 slice. The times are simulated.
16 devices in a mesh: rep: 2 (over y, z), dp: 8 (over x, core).
Axes of the slice: x: 4, y: 2, z: 1, core: 2. Of those that a mesh axis runs over, the one named last changes fastest.
The devices are a block of a 4x4x8 slice.
Arguments:
- x: bfloat16 [16, 2048, 1536], P(('rep', 'dp')), parts along dimension 0
- dy: bfloat16 [16, 2048, 1536], P(('rep', 'dp')), parts along dimension 0
- w_gate: bfloat16 [2, 1536, 4224], P(None, 'dp')
- w_up: bfloat16 [2, 1536, 4224], P(None, 'dp')
- w_down: bfloat16 [2, 4224, 1536], P(None, 'dp')
- m_w_gate: float32 [2, 1536, 4224], P(None, 'dp')
- m_w_up: float32 [2, 1536, 4224], P(None, 'dp')
- m_w_down: float32 [2, 4224, 1536], P(None, 'dp')
- v_w_gate: float32 [2, 1536, 4224], P(None, 'dp')
- v_w_up: float32 [2, 1536, 4224], P(None, 'dp')
- v_w_down: float32 [2, 4224, 1536], P(None, 'dp')
Outputs:
- output 1: bfloat16 [4, 1536, 4224], P('rep', 'dp'), parts along dimension 0
- output 2: bfloat16 [4, 1536, 4224], P('rep', 'dp'), parts along dimension 0
- output 3: bfloat16 [4, 4224, 1536], P('rep', 'dp'), parts along dimension 0
- output 4: float32 [4, 1536, 4224], P('rep', 'dp'), parts along dimension 0
- output 5: float32 [4, 1536, 4224], P('rep', 'dp'), parts along dimension 0
- output 6: float32 [4, 4224, 1536], P('rep', 'dp'), parts along dimension 0
- output 7: float32 [4, 1536, 4224], P('rep', 'dp'), parts along dimension 0
- output 8: float32 [4, 1536, 4224], P('rep', 'dp'), parts along dimension 0
- output 9: float32 [4, 4224, 1536], P('rep', 'dp'), parts along dimension 0
There are 2 independent parts. A program takes and returns all parts, laid end to end along the dimension named above; an argument that names none is the same for every part.
All inputs are finite; a program needn't handle non-finite values.
Results may differ from a plain program's by a relative error of at most 0.022.
Values are sent between devices in bfloat16 or wider.
A program may use at most 768 MiB of HBM per device.

v0:
```python
import jax
import jax.numpy as jnp
from jax import lax
from jax.sharding import PartitionSpec as P

NAMES = ("w_gate", "w_up", "w_down")


def matmul(a, w):
    return jnp.dot(a, w, preferred_element_type=jnp.float32).astype(jnp.bfloat16)


def normed(h):
    wide = h.astype(jnp.float32)
    scale = lax.rsqrt(jnp.mean(wide**2, -1, keepdims=True) + 1e-6)
    return (wide * scale).astype(jnp.bfloat16)


def layer(h, w):
    a = normed(h)
    gate = jnp.dot(a, w["w_gate"], preferred_element_type=jnp.float32)
    up = jnp.dot(a, w["w_up"], preferred_element_type=jnp.float32)
    return h + matmul((jax.nn.silu(gate) * up).astype(jnp.bfloat16), w["w_down"])


def adamw(w, m, v, g):
    m = 0.9 * m + 0.1 * g
    v = 0.95 * v + 0.05 * g * g
    step = m * lax.rsqrt(v + 1e-8) + 0.1 * w
    return (w - 0.02 * step).astype(jnp.bfloat16), m, v


def clipped(gradients, sum_of_squares, count):
    factor = jnp.minimum(1.0, 0.5 * lax.rsqrt(sum_of_squares / count + 1e-30))
    return [g * factor for g in gradients]


def solution(mesh):
    def fetched(weights, number):
        return {name: lax.all_gather(w[number], "dp", axis=0, tiled=True) for name, w in zip(NAMES, weights, strict=True)}

    def step(x, dy, *arrays):
        weights, m, v = (arrays[i : i + 3] for i in (0, 3, 6))
        layers = weights[0].shape[0]
        h, kept = x[0], []
        for number in range(layers):
            kept.append(h)
            h = layer(h, fetched(weights, number))
        by_h, mine = dy[0], [None] * layers
        for number in reversed(range(layers)):
            _, back = jax.vjp(lambda w, h: layer(h, w), fetched(weights, number), kept[number])
            by_w, by_h = back(by_h)
            mine[number] = [lax.psum_scatter(by_w[name], "dp", scatter_dimension=0, tiled=True) for name in NAMES]
        gradients = [jnp.stack([mine[number][i] for number in range(layers)]).astype(jnp.float32) for i in range(3)]
        squares = lax.psum(sum(jnp.sum(g * g) for g in gradients), "dp")
        gradients = clipped(gradients, squares, lax.psum(1, "dp") * sum(g.size for g in gradients))
        new = [adamw(w.astype(jnp.float32), m, v, g) for w, m, v, g in zip(weights, m, v, gradients, strict=True)]
        return tuple(one[which] for which in range(3) for one in new)

    states, cut = P(("rep", "dp"), None, None), P(None, "dp", None)
    return jax.shard_map(
        step,
        mesh=mesh,
        in_specs=(states, states) + (cut,) * 9,
        out_specs=(P("rep", "dp", None),) * 9,
        check_vma=False,
    )
```

profile of v0, /device:TPU:112, one launch (start us, length us, event | category | flops | bytes accessed | tf_op | source)
XLA Modules:
  0.0 1093.1 jit_solution(3040452152007542606)
XLA Ops:
  7.3 4.0 fusion.102
  11.3 0.1 all-gather.15.cloned.1.call-start
  11.4 1.9 fusion.101
  13.4 3.8 fusion.100
  17.4 0.6 all-gather.21.cloned.1.call-update
  18.0 0.6 all-gather.23.cloned.1.call-update
  18.7 0.6 all-gather.19.cloned.1.call-update
  19.3 8.6 copy.20
  27.9 4.1 fusion.34
  32.1 8.6 copy.21
  40.7 38.6 %all-gather.13.cloned.1.call-done = bf16[1,1536,4224]{2,1,0:T(8,128)(2,1)} async-done(((bf16[1,192,4224]{2,1,0:T(8,128)(2,1)}), bf16[1,1536,4224]{2,1,0:T(8,128)(2,1)}) %all-gather.13.cloned.1.call-update) | async-done | bytes 12976144 | tf_op jit(solution)/shard_map/all_gather | solution.py:40
  79.2 37.3 %fusion.32 = f32[2048,4224]{1,0:T(8,128)} fusion(bf16[1,1536,4224]{2,1,0:T(8,128)(2,1)} %all-gather.13.cloned.1.call-done, bf16[1,2048,1536]{1,2,0:T(8,128)(2,1)} %copy.20, f32[2048]{0:T(1024)S(1)} %add_rsqrt_fusion), kind=kOutput, calls=%fused_computation.51 | convolution fusion | flops 26584547328 | bytes 53878784 | tf_op jit(solution)/shard_map/dot_general | solution.py:21
  116.6 30.2 %all-gather.15.cloned.1.call-done = bf16[1,1536,4224]{2,1,0:T(8,128)(2,1)} async-done(((bf16[1,192,4224]{2,1,0:T(8,128)(2,1)}), bf16[1,1536,4224]{2,1,0:T(8,128)(2,1)}) %all-gather.15.cloned.1.call-update) | async-done | bytes 12976144 | tf_op jit(solution)/shard_map/all_gather | solution.py:40
  146.7 48.3 %multiply_convert_fusion.1 = (bf16[2048,4224]{1,0:T(8,128)(2,1)}, f32[2048,4224]{1,0:T(8,128)}) fusion(f32[2048,4224]{1,0:T(8,128)} %fusion.32, bf16[1,1536,4224]{2,1,0:T(8,128)(2,1)} %all-gather.15.cloned.1.call-done, bf16[1,2048,1536]{1,2,0:T(8,128)(2,1)} %copy.20, f32[2048]{0:T(1024)S(1)} %add_rsqrt_fusion), kind=kOutput, calls=%fused_computation.17 | convolution fusion | flops 26636451840 | bytes 105783296 | tf_op jit(solution)/shard_map/dot_general | solution.py:22
  195.1 19.2 %all-gather.17.cloned.1.call-done = bf16[1,4224,1536]{2,1,0:T(8,128)(2,1)} async-done(((bf16[1,528,1536]{2,1,0:T(8,128)(2,1)}), bf16[1,4224,1536]{2,1,0:T(8,128)(2,1)}) %all-gather.17.cloned.1.call-update) | async-done | bytes 12976144 | tf_op jit(solution)/shard_map/all_gather | solution.py:40
  214.3 48.9 %fusion.38 = (f32[2048]{0:T(1024)S(1)}, bf16[2048,1536]{0,1:T(8,128)(2,1)}) fusion(bf16[2048,4224]{1,0:T(8,128)(2,1)} %get-tuple-element.24, bf16[1,4224,1536]{2,1,0:T(8,128)(2,1)} %all-gather.17.cloned.1.call-done, bf16[1,2048,1536]{1,2,0:T(8,128)(2,1)} %copy.20), kind=kOutput, calls=%fused_computation.57 | convolution fusion | flops 26590836736 | bytes 42868736 | tf_op jit(solution)/shard_map/dot_general | solution.py:10
  263.2 0.6 copy-done.8
  263.8 17.8 %all-gather.21.cloned.1.call-done = bf16[1,4224,1536]{2,1,0:T(8,128)(2,1)} async-done(((bf16[1,528,1536]{2,1,0:T(8,128)(2,1)}), bf16[1,4224,1536]{2,1,0:T(8,128)(2,1)}) %all-gather.21.cloned.1.call-update) | async-done | bytes 12976144 | tf_op jit(solution)/shard_map/all_gather | solution.py:40
  281.6 35.7 %convolution_convert_fusion.2 = bf16[2048,4224]{1,0:T(8,128)(2,1)} fusion(bf16[1,4224,1536]{2,1,0:T(8,128)(2,1)} %all-gather.21.cloned.1.call-done, bf16[1,2048,1536]{2,1,0:T(8,128)(2,1)} %param.12), kind=kOutput, calls=%fused_computation.31 | convolution fusion | flops 26583760896 | bytes 36569088 | tf_op jit(solution)/shard_map/transpose(jvp())/dot_general | solution.py:10
  317.3 31.7 %all-gather.23.cloned.1.call-done = bf16[1,1536,4224]{2,1,0:T(8,128)(2,1)} async-done(((bf16[1,192,4224]{2,1,0:T(8,128)(2,1)}), bf16[1,1536,4224]{2,1,0:T(8,128)(2,1)}) %all-gather.23.cloned.1.call-update) | async-done | bytes 12976144 | tf_op jit(solution)/shard_map/all_gather | solution.py:40
  349.0 37.4 %fusion.19 = f32[2048,4224]{1,0:T(8,128)} fusion(bf16[1,1536,4224]{2,1,0:T(8,128)(2,1)} %all-gather.23.cloned.1.call-done, bf16[2048,1536]{0,1:T(8,128)(2,1)} %get-tuple-element.27, f32[2048]{0:T(1024)S(1)} %fusion.88), kind=kOutput, calls=%fused_computation.38 | convolution fusion | flops 26584547328 | bytes 53878784 | tf_op jit(solution)/shard_map/jvp()/dot_general | solution.py:22
  386.4 30.0 %all-gather.19.cloned.1.call-done = bf16[1,1536,4224]{2,1,0:T(8,128)(2,1)} async-done(((bf16[1,192,4224]{2,1,0:T(8,128)(2,1)}), bf16[1,1536,4224]{2,1,0:T(8,128)(2,1)}) %all-gather.19.cloned.1.call-update) | async-done | bytes 12976144 | tf_op jit(solution)/shard_map/all_gather | solution.py:40
  416.3 55.6 %fusion.2 = (bf16[2048,4224]{1,0:T(8,128)(2,1)}, f32[2048,4224]{1,0:T(8,128)}) fusion(f32[2048,4224]{1,0:T(8,128)} %fusion.19, bf16[2048,4224]{1,0:T(8,128)(2,1)} %convolution_convert_fusion.2, bf16[1,1536,4224]{2,1,0:T(8,128)(2,1)} %all-gather.19.cloned.1.call-done, bf16[2048,1536]{0,1:T(8,128)(2,1)} %get-tuple-element.27, f32[2048]{0:T(1024)S(1)} %fusion.88), kind=kOutput, calls=%fused_computation.8 | convolution fusion | flops 26688356352 | bytes 123084800 | tf_op jit(solution)/shard_map/jvp()/dot_general | solution.py:21
  471.9 36.0 %fusion.47 = bf16[2048,1536]{0,1:T(8,128)(2,1)} fusion(bf16[2048,4224]{1,0:T(8,128)(2,1)} %get-tuple-element.28, bf16[1,1536,4224]{2,1,0:T(8,128)(2,1)} %all-gather.19.cloned.1.call-done), kind=kOutput, calls=%fused_computation.79 | convolution fusion | flops 26575110144 | bytes 36569088 | tf_op jit(solution)/shard_map/transpose(jvp())/dot_general | solution.py:21
  508.0 44.8 %fusion.40 = (f32[2048]{0:T(1024)S(1)}, bf16[2048,1536]{0,1:T(8,128)(2,1)}) fusion(bf16[2048,1536]{0,1:T(8,128)(2,1)} %get-tuple-element.27, bf16[2048,1536]{0,1:T(8,128)(2,1)} %fusion.47, bf16[1,1536,4224]{2,1,0:T(8,128)(2,1)} %all-gather.23.cloned.1.call-done, bf16[2048,4224]{1,0:T(8,128)(2,1)} %convolution_convert_fusion.2, ...), kind=kOutput, calls=%fused_computation.59 | convolution fusion | flops 26645886976 | bytes 83763200 | tf_op jit(solution)/shard_map/transpose(jvp())/dot_general | solution.py:22
  552.8 8.6 fusion.71
  561.4 2.7 copy-done.4
  564.1 32.9 %convolution_convert_fusion.4 = bf16[4224,1536]{1,0:T(8,128)(2,1)} fusion(bf16[2048,4224]{1,0:T(8,128)(2,1)} %get-tuple-element.24, bf16[2048,1536]{0,1:T(8,128)(2,1)S(1)} %fusion.71), kind=kOutput, calls=%fused_computation.33 | convolution fusion | flops 26581598208 | bytes 36569088 | tf_op jit(solution)/shard_map/transpose(jvp())/dot_general | solution.py:10
  597.1 0.1 reduce-scatter.17.cloned.1.call-start
  597.2 39.5 %convolution_convert_fusion.3 = bf16[4224,1536]{1,0:T(8,128)(2,1)} fusion(f32[2048,4224]{1,0:T(8,128)} %fusion.19, bf16[1,2048,1536]{2,1,0:T(8,128)(2,1)} %param.12, f32[2048,4224]{1,0:T(8,128)} %get-tuple-element.29), kind=kOutput, calls=%fused_computation.32 | convolution fusion | flops 26633502720 | bytes 88473600 | tf_op jit(solution)/shard_map/transpose(jvp())/dot_general | solution.py:10
  636.7 0.1 reduce-scatter.11.cloned.1.call-start
  636.8 35.9 %convolution_convert_fusion.1 = bf16[2048,4224]{1,0:T(8,128)(2,1)} fusion(bf16[2048,1536]{0,1:T(8,128)(2,1)} %copy-done.4, bf16[1,4224,1536]{2,1,0:T(8,128)(2,1)} %all-gather.17.cloned.1.call-done), kind=kOutput, calls=%fused_computation.30 | convolution fusion | flops 26583760896 | bytes 36569088 | tf_op jit(solution)/shard_map/transpose(jvp())/dot_general | solution.py:10
  672.7 43.3 %fusion.17 = bf16[1536,4224]{1,0:T(8,128)(2,1)} fusion(bf16[2048,4224]{1,0:T(8,128)(2,1)} %convolution_convert_fusion.1, f32[2048,4224]{1,0:T(8,128)} %fusion.32, bf16[1,2048,1536]{1,2,0:T(8,128)(2,1)} %copy.20, f32[2048]{0:T(1024)S(1)} %copy-done.11), kind=kOutput, calls=%fused_computation.28 | convolution fusion | flops 26642939904 | bytes 71180288 | tf_op jit(solution)/shard_map/transpose(jvp())/dot_general | solution.py:22
  716.1 0.1 reduce-scatter.13.cloned.1.call-start
  716.2 0.6 copy-done.7
  716.7 42.9 %fusion.13 = bf16[1536,4224]{1,0:T(8,128)(2,1)} fusion(bf16[2048,4224]{1,0:T(8,128)(2,1)} %convolution_convert_fusion.2, bf16[2048,1536]{0,1:T(8,128)(2,1)} %get-tuple-element.27, f32[2048]{0:T(1024)S(1)} %copy-done.7, f32[2048,4224]{1,0:T(8,128)} %get-tuple-element.29), kind=kOutput, calls=%fused_computation.26 | convolution fusion | flops 26642939904 | bytes 71180288 | tf_op jit(solution)/shard_map/transpose(jvp())/dot_general | solution.py:22
  759.8 45.5 %fusion.14 = bf16[1536,4224]{1,0:T(8,128)(2,1)} fusion(f32[2048,4224]{1,0:T(8,128)} %fusion.32, f32[2048,4224]{1,0:T(8,128)} %get-tuple-element.25, bf16[2048,4224]{1,0:T(8,128)(2,1)} %convolution_convert_fusion.1, bf16[1,2048,1536]{1,2,0:T(8,128)(2,1)} %copy.20, f32[2048]{0:T(1024)S(1)} %copy-done.11), kind=kOutput, calls=%fused_computation.27 | convolution fusion | flops 26686193664 | bytes 105783296 | tf_op jit(solution)/shard_map/transpose(jvp())/dot_general | solution.py:21
  805.4 0.1 reduce-scatter.9.cloned.1.call-start
  805.4 35.8 %convolution_convert_fusion = bf16[1536,4224]{1,0:T(8,128)(2,1)} fusion(bf16[2048,4224]{1,0:T(8,128)(2,1)} %get-tuple-element.28, bf16[2048,1536]{0,1:T(8,128)(2,1)} %get-tuple-element.27, f32[2048]{0:T(1024)S(1)} %copy-done.7), kind=kOutput, calls=%fused_computation.29 | convolution fusion | flops 26584547328 | bytes 36577280 | tf_op jit(solution)/shard_map/transpose(jvp())/dot_general | solution.py:21
  841.3 4.3 fusion.61
  845.7 38.8 %reduce-scatter.13.cloned.1.call-done = bf16[192,4224]{1,0:T(8,128)(2,1)} async-done(((bf16[1536,4224]{1,0:T(8,128)(2,1)}), bf16[192,4224]{1,0:T(8,128)(2,1)}) %reduce-scatter.13.cloned.1.call-update) | async-done | bytes 1622032 | tf_op jit(solution)/shard_map/reduce_scatter | solution.py:53
  884.5 4.2 fusion.60
  888.7 68.1 %reduce-scatter.7.cloned.1.call-done = bf16[192,4224]{1,0:T(8,128)(2,1)} async-done(((bf16[1536,4224]{1,0:T(8,128)(2,1)}), bf16[192,4224]{1,0:T(8,128)(2,1)}) %reduce-scatter.7.cloned.1.call-update) | async-done | bytes 1622032 | tf_op jit(solution)/shard_map/reduce_scatter | solution.py:53
  956.7 72.1 %reduce-scatter.9.cloned.1.call-done = bf16[192,4224]{1,0:T(8,128)(2,1)} async-done(((bf16[1536,4224]{1,0:T(8,128)(2,1)}), bf16[192,4224]{1,0:T(8,128)(2,1)}) %reduce-scatter.9.cloned.1.call-update) | async-done | bytes 1622032 | tf_op jit(solution)/shard_map/reduce_scatter | solution.py:53
  1028.8 4.2 fusion.59
  1035.0 13.3 %psum.7 = f32[]{:T(128)} all-reduce(f32[]{:T(128)S(6)} %add.99), channel_id=1, replica_groups=mesh['rep'=2,'dp'=8] {'dp'}, use_global_device_ids=true, to_apply=%region_12.13 | all-reduce | flops 1 | bytes 8 | tf_op jit(solution)/shard_map/psum | solution.py:55
  1049.0 11.9 %fusion.67 = (bf16[2,528,1536]{2,1,0:T(8,128)(2,1)}, f32[2,528,1536]{2,1,0:T(8,128)}, f32[2,528,1536]{2,1,0:T(8,128)}) fusion(bf16[2,528,1536]{2,1,0:T(8,128)(2,1)S(1)} %copy-done.3, f32[]{:T(128)S(6)} %min_shard_map.3, bf16[1,528,1536]{2,1,0:T(8,128)(2,1)} %bitcast.79, bf16[1,528,1536]{2,1,0:T(8,128)(2,1)} %bitcast.77, f32[2,528,1536]{2,1,0:T(8,128)} %param.21, ...), kind=kLoop, calls=%fused_computation.95 | loop fusion | flops 32440320 | bytes 35684356 | tf_op jit(solution)/shard_map/convert_element_type | solution.py:30
  1060.9 24.8 %fusion.58 = (bf16[2,192,4224]{2,1,0:T(8,128)(2,1)}, f32[2,192,4224]{2,1,0:T(8,128)}, f32[2,192,4224]{2,1,0:T(8,128)}, bf16[2,192,4224]{2,1,0:T(8,128)(2,1)}, f3...) fusion(bf16[2,192,4224]{2,1,0:T(8,128)(2,1)S(1)} %copy-done, f32[]{:T(128)S(6)} %min_shard_map.3, ...), kind=kLoop, calls=%fused_computation.86 | loop fusion | flops 64880640 | bytes 71368704 | tf_op jit(solution)/shard_map/convert_element_type | solution.py:30
  (43 shorter events, 1.0 us)
Async XLA Ops:
  7.2 4.2 copy-start.1
  7.2 72.0 %all-gather.13.cloned.1.call-start = ((), (), s32[]{:S(2)}) async-start(), calls=%async_computation.12 | async-start | bytes 14598144 | tf_op jit(solution)/shard_map/all_gather | solution.py:40
  11.3 135.4 %all-gather.15.cloned.1.call-start = ((), (), s32[]{:S(2)}) async-start(), calls=%async_computation.13 | async-start | bytes 14598144 | tf_op jit(solution)/shard_map/all_gather | solution.py:40
  13.4 200.9 %all-gather.17.cloned.1.call-start = ((), (), s32[]{:S(2)}) async-start(), calls=%async_computation.14 | async-start | bytes 14598144 | tf_op jit(solution)/shard_map/all_gather | solution.py:40
  17.3 264.3 %all-gather.21.cloned.1.call-start = ((), (), s32[]{:S(2)}) async-start(), calls=%async_computation.16 | async-start | bytes 14598144 | tf_op jit(solution)/shard_map/all_gather | solution.py:40
  18.0 331.0 %all-gather.23.cloned.1.call-start = ((), (), s32[]{:S(2)}) async-start(), calls=%async_computation.17 | async-start | bytes 14598144 | tf_op jit(solution)/shard_map/all_gather | solution.py:40
  18.6 397.7 %all-gather.19.cloned.1.call-start = ((), (), s32[]{:S(2)}) async-start(), calls=%async_computation.15 | async-start | bytes 14598144 | tf_op jit(solution)/shard_map/all_gather | solution.py:40
  19.2 822.0 %reduce-scatter.15.cloned.1.call-start = ((), (), s32[]{:S(2)}) async-start(), calls=%async_computation.10 | async-start | bytes 14598144 | tf_op jit(solution)/shard_map/reduce_scatter | solution.py:53
  32.0 114.7 %copy-start.10 = (f32[2048]{0:T(1024)}, f32[2048]{0:T(1024)S(1)}, u32[]{:S(2)}) copy-start(f32[2048]{0:T(1024)S(1)} %add_rsqrt_fusion) | copy-start | bytes 24580
  263.2 0.6 copy-start.8
  263.8 152.5 %copy-start.5 = (f32[2048]{0:T(1024)}, f32[2048]{0:T(1024)S(1)}, u32[]{:S(2)}) copy-start(f32[2048]{0:T(1024)S(1)} %fusion.88) | copy-start | bytes 24580
  508.0 44.8 %copy-start.9 = (f32[2048]{0:T(1024)S(1)}, f32[2048]{0:T(1024)}, u32[]{:S(2)}) copy-start(f32[2048]{0:T(1024)} %copy-done.8) | copy-start | bytes 24580
  508.0 44.9 %copy-start.6 = (f32[2048]{0:T(1024)S(1)}, f32[2048]{0:T(1024)}, u32[]{:S(2)}) copy-start(f32[2048]{0:T(1024)} %copy-done.5) | copy-start | bytes 24580
  561.4 2.7 copy-start.4
  597.1 244.2 %reduce-scatter.17.cloned.1.call-start = ((), (), s32[]{:S(2)}) async-start(), calls=%async_computation.11 | async-start | bytes 14598144 | tf_op jit(solution)/shard_map/reduce_scatter | solution.py:53
  636.7 36.0 %copy-start.11 = (f32[2048]{0:T(1024)S(1)}, f32[2048]{0:T(1024)}, u32[]{:S(2)}) copy-start(f32[2048]{0:T(1024)} %copy-done.10) | copy-start | bytes 24580
  636.7 208.9 %reduce-scatter.11.cloned.1.call-start = ((), (), s32[]{:S(2)}) async-start(), calls=%async_computation.8 | async-start | bytes 14598144 | tf_op jit(solution)/shard_map/reduce_scatter | solution.py:53
  716.0 0.7 copy-start.7
  716.1 168.4 %reduce-scatter.13.cloned.1.call-start = ((), (), s32[]{:S(2)}) async-start(), calls=%async_computation.9 | async-start | bytes 14598144 | tf_op jit(solution)/shard_map/reduce_scatter | solution.py:53
  759.7 197.0 %reduce-scatter.7.cloned.1.call-start = ((), (), s32[]{:S(2)}) async-start(), calls=%async_computation.6 | async-start | bytes 14598144 | tf_op jit(solution)/shard_map/reduce_scatter | solution.py:53
  805.4 223.5 %reduce-scatter.9.cloned.1.call-start = ((), (), s32[]{:S(2)}) async-start(), calls=%async_computation.7 | async-start | bytes 14598144 | tf_op jit(solution)/shard_map/reduce_scatter | solution.py:53
  841.3 207.7 %copy-start.3 = (bf16[2,528,1536]{2,1,0:T(8,128)(2,1)S(1)}, bf16[2,528,1536]{2,1,0:T(8,128)(2,1)}, u32[]{:S(2)}) copy-start(bf16[2,528,1536]{2,1,0:T(8,128)(2,1)} %param.15) | copy-start | bytes 9732100
  1049.0 11.9 %copy-start = (bf16[2,192,4224]{2,1,0:T(8,128)(2,1)S(1)}, bf16[2,192,4224]{2,1,0:T(8,128)(2,1)}, u32[]{:S(2)}) copy-start(bf16[2,192,4224]{2,1,0:T(8,128)(2,1)} %param.13) | copy-start | bytes 9732100
  1049.0 11.9 %copy-start.2 = (bf16[2,192,4224]{2,1,0:T(8,128)(2,1)S(1)}, bf16[2,192,4224]{2,1,0:T(8,128)(2,1)}, u32[]{:S(2)}) copy-start(bf16[2,192,4224]{2,1,0:T(8,128)(2,1)} %param.14) | copy-start | bytes 9732100
Sparse Core Ops, SparseCore 0:
  11.4 67.7 all-gather.12
  81.4 65.3 all-gather.14
  148.9 65.3 all-gather.16
  216.3 65.3 all-gather.20
  283.6 65.3 all-gather.22
  351.0 65.3 all-gather.18
  597.2 70.5 reduce-scatter.14
  670.2 69.9 reduce-scatter.16
  742.5 69.8 reduce-scatter.10
  814.6 69.8 reduce-scatter.12
  886.8 69.8 reduce-scatter.6
  958.9 69.8 reduce-scatter.8
where the time goes:
time: 1100 us; the launch traced here: 1090 us
  matrix products  620 us (56%)
  waiting for transfers between devices  349 us (32%)
  other arithmetic  62.1 us (6%)
  local copies, waits for them, and re-layouts  30.9 us (3%)
  between operations  17.5 us (2%)
  blocking collectives  13.3 us (1%)
    dot_general x5, matrix products, layer(): up = jnp.dot(a, w['w_up'], preferred_element_type=jnp.float32)  217 us
    dot_general x5, matrix products, layer(): gate = jnp.dot(a, w['w_gate'], preferred_element_type=jnp.float32)  210 us
    dot_general x5, matrix products, matmul(): jnp.dot(a, w, preferred_element_type=jnp.float32).astype(jnp.bfloat16)  193 us
    reduce_scatter x6, waiting for transfers between devices, step(): lax.psum_scatter(by_w[name], 'dp', scatter_dimension=0, tiled=True)  179 us
    all_gather x6, waiting for transfers between devices, fetched(): lax.all_gather(w[number], 'dp', axis=0, tiled=True)  167 us
    convert_element_type x2, other arithmetic, adamw(): return ((w - 0.02 * step).astype(jnp.bfloat16), m, v)  36.7 us
  transfers between devices with their start and end apart: 12, of which 9 were waited for; matrix products, arithmetic and copies ran while one was open for 44% of the time, Pallas kernels for 0%

commit v1 on v0

v1 whole, which is shorter than its diff:
```python
import functools
import jax, jax.numpy as jnp
from jax import lax
from jax.experimental import pallas as pl
from jax.experimental.pallas import tpu as pltpu
from jax.sharding import PartitionSpec as P
MESH=pl.DeviceIdType.MESH
BF, F32 = jnp.bfloat16, jnp.float32
VMEM_LIMIT = 67043328

def norm_of(wide):
    return (wide * lax.rsqrt(jnp.mean(wide * wide, -1, keepdims=True) + 1e-6)).astype(BF)

TN = 256
TB = 512
CH = 512

def fwd_kernel(n, x, wg, wu, wd, WG, WU, WD, GATE, UP, HIDT, AT, H1,
               a_v, wbuf, wtail, gbuf, ubuf, hbuf, gtail, utail, htail, wd_v, htbuf, xbuf, h1buf, atbuf, bounce, bounced,
               send, recv, w_sem, g_sem, u_sem, h_sem, wd_sem, ht_sem, x_sem, h1_sem, at_sem, b_sem, b_out):
    T, D = x.shape
    F = wg.shape[2]
    full = F // TN
    rest = F - full * TN
    r, me = lax.axis_index("rep"), lax.axis_index("dp")
    right, left = lax.rem(me + 2, n), lax.rem(me + n - 2, n)
    across = lax.rem(me + n // 2, n)
    odd = lax.rem(me, 2)
    sib = me + 1 - 2 * odd
    par = lax.rem(r, 2)
    partner = r + 1 - 2 * par
    to = {"R": (r, right), "L": (r, left), "S": (r, sib), "Y": (partner, me)}

    def twin(d):
        return d + 1 - 2 * odd

    shards = [(wg, WG, 0), (wu, WU, 0), (wd, WD, 0), (wg, WG, 1), (wu, WU, 1), (wd, WD, 1)]

    def moves(m):
        w, W, l = shards[m]
        R = w.shape[1]
        c = R // 3
        N, P1, P2, ALL = (0, c), (c * (1 + par), c), (c * (2 - par), c), (0, R)
        return {
            "rN": (me, N, "R", True), "lP": (me, P1, "L", True), "rP": (me, P1, "R", True), "lN": (me, N, "L", True),
            "sO": (me, ALL, "S", True),
            "oN": (left, N, "R", False), "oP": (right, P1, "L", False),
            "ylP": (right, P1, "Y", False), "yrP": (left, P1, "Y", False), "yoP": (across, P1, "Y", False),
            "srN": (left, N, "S", False), "srP": (left, P1, "S", False), "slP": (right, P1, "S", False), "slN": (right, N, "S", False),
            "soN": (across, N, "S", False), "soP": (across, P1, "S", False),
            "syl": (right, P2, "S", False), "syr": (left, P2, "S", False), "syo": (across, P2, "S", False),
        }

    ORDER = list(moves(0))

    def copy(m, name):
        w, W, l = shards[m]
        R = w.shape[1]
        owner, (first, rows), way, own = moves(m)[name]
        there = W.at[l, pl.ds(pl.multiple_of(owner * R + first, 8), rows)]
        src = w.at[l, pl.ds(pl.multiple_of(first, 8) if not isinstance(first, int) else first, rows)] if own else there
        k = ORDER.index(name)
        return pltpu.make_async_remote_copy(src_ref=src, dst_ref=there, send_sem=send.at[m, k], recv_sem=recv.at[m, k],
                                            device_id=to[way], device_id_type=MESH)

    def start(m, *names):
        for name in names:
            copy(m, name).start()

    def arrive(m, *names):
        for name in names:
            copy(m, name).wait_recv()

    def e1(m): start(m, "rN", "lP", "rP", "lN", "sO")
    def e2(m):
        arrive(m, "rN", "lP"); start(m, "oN", "oP", "ylP", "srN", "slP")
    def e3(m):
        arrive(m, "rP", "lN"); start(m, "yrP", "srP", "slN")
    def e4(m):
        arrive(m, "oN", "oP", "ylP"); start(m, "yoP", "soN", "soP", "syl")
    def e5(m):
        arrive(m, "yrP"); start(m, "syr")
    def e6(m):
        arrive(m, "yoP"); start(m, "syo")
    def e7(m):
        arrive(m, "sO", "srN", "srP", "slP", "slN", "soN", "soP", "syl", "syr", "syo")

    M = len(shards)
    def tick(t):
        m, phase = divmod(t, 3)
        if phase == 0:
            if 0 <= m - 1 < M: e4(m - 1); e5(m - 1)
        elif phase == 1:
            if m < M: e2(m)
            if 0 <= m - 1 < M: e6(m - 1)
        else:
            if m < M: e3(m)
            if m + 1 < M: e1(m + 1)

    barrier = pltpu.get_barrier_semaphore()
    for way in to:
        pl.semaphore_signal(barrier, inc=1, device_id=to[way], device_id_type=MESH)
    pl.semaphore_wait(barrier, 4)
    e1(0)

    def slot_of(m):
        w, W, l = shards[m]
        return bounced if w is wd else bounce
    def own_in(m):
        w, W, l = shards[m]
        return pltpu.make_async_copy(w.at[l], slot_of(m), b_sem.at[m])
    def own_out(m):
        w, W, l = shards[m]
        R = w.shape[1]
        return pltpu.make_async_copy(slot_of(m), W.at[l, pl.ds(pl.multiple_of(me * R, 8), R)], b_out.at[m])
    own_in(0).start(); own_in(2).start()

    nb = T // TB
    def x_in(i, s): return pltpu.make_async_copy(x.at[pl.ds(i * TB, TB)], xbuf.at[s], x_sem.at[s])
    def at_out(l, i, s): return pltpu.make_async_copy(atbuf.at[s], AT.at[l, :, pl.ds(i * TB, TB)], at_sem.at[s])
    def h1_out(i, s): return pltpu.make_async_copy(h1buf.at[s], H1.at[pl.ds(i * TB, TB)], h1_sem.at[s])
    def put_a(l, i, s, wide):
        a = norm_of(wide)
        a_v[pl.ds(i * TB, TB)] = a
        atbuf[s] = a.T
        at_out(l, i, s).start()
    x_in(0, 0).start()
    for i in range(nb):
        s = i % 2
        x_in(i, s).wait()
        if i + 1 < nb: x_in(i + 1, 1 - s).start()
        if i >= 2: at_out(0, i - 2, s).wait()
        put_a(0, i, s, xbuf[s].astype(F32))
    for i in (nb - 2, nb - 1): at_out(0, i, i % 2).wait()
    own_in(2).wait(); own_out(2).start()
    for m, after in ((0, 1), (1, 3), (3, 4), (4, None)):
        own_in(m).wait(); own_out(m).start(); own_out(m).wait()
        if after is not None: own_in(after).start()
        if m == 0:
            own_out(2).wait(); own_in(5).start()
    own_in(5).wait(); own_out(5).start(); own_out(5).wait()

    for t in (1, 2, 3, 4): tick(t)

    def cols(j): return pl.ds(pl.multiple_of(j * TN, TN), TN)
    LAST = pl.ds(full * TN, rest)

    def columns_phase(W, l, up, ticks):
        def w_in(j, s): return pltpu.make_async_copy(W.at[l, :, cols(j)], wbuf.at[s], w_sem.at[s])
        def w_in_last(): return pltpu.make_async_copy(W.at[l, :, LAST], wtail, w_sem.at[2])
        def g_in(j, s): return pltpu.make_async_copy(GATE.at[l, :, cols(j)], gbuf.at[s], g_sem.at[s])
        def g_in_last(): return pltpu.make_async_copy(GATE.at[l, :, LAST], gtail, g_sem.at[2])
        def g_out(j, s): return pltpu.make_async_copy(gbuf.at[s], GATE.at[l, :, cols(j)], g_sem.at[s])
        def g_out_last(): return pltpu.make_async_copy(gtail, GATE.at[l, :, LAST], g_sem.at[2])
        def u_out(j, s): return pltpu.make_async_copy(ubuf.at[s], UP.at[l, :, cols(j)], u_sem.at[s])
        def u_out_last(): return pltpu.make_async_copy(utail, UP.at[l, :, LAST], u_sem.at[2])
        def h_out(j, s): return pltpu.make_async_copy(hbuf.at[s], HIDT.at[l, cols(j)], h_sem.at[s])
        def h_out_last(): return pltpu.make_async_copy(htail, HIDT.at[l, LAST], h_sem.at[2])

        def compute(w_ref, g_ref, u_ref, h_ref):
            for c in range(T // CH):
                rows = pl.ds(c * CH, CH)
                got = jnp.dot(a_v[rows], w_ref[...], preferred_element_type=F32)
                if not up:
                    g_ref[rows] = got
                else:
                    g = g_ref[rows]
                    u_ref[rows] = got
                    hid = (g * (1 / (1 + jnp.exp(-g))) * got).astype(BF)
                    h_ref[:, rows] = hid.T

        w_in(0, 0).start()
        if up: g_in(0, 0).start()
        def step(j, carry):
            s = lax.rem(j, 2)
            for at, t in ticks.items():
                if at < full:
                    @pl.when(j == at)
                    def _(): tick(t)
            w_in(j, s).wait()
            if up: g_in(j, s).wait()
            @pl.when(j + 1 < full)
            def _():
                w_in(j + 1, 1 - s).start()
                if up: g_in(j + 1, 1 - s).start()
            @pl.when(j + 1 == full)
            def _():
                w_in_last().start()
                if up: g_in_last().start()
            @pl.when(j >= 2)
            def _():
                if up:
                    u_out(j - 2, s).wait(); h_out(j - 2, s).wait()
                else:
                    g_out(j - 2, s).wait()
            compute(wbuf.at[s], gbuf.at[s], ubuf.at[s], hbuf.at[s])
            if up:
                u_out(j, s).start(); h_out(j, s).start()
            else:
                g_out(j, s).start()
            return carry
        lax.fori_loop(0, full, step, 0)
        w_in_last().wait()
        if up: g_in_last().wait()
        compute(wtail, gtail, utail, htail)
        if up:
            u_out_last().start(); h_out_last().start()
        else:
            g_out_last().start()
        for at, t in ticks.items():
            if at >= full: tick(t)
        for j in (full - 2, full - 1):
            if up:
                u_out(j, j % 2).wait(); h_out(j, j % 2).wait()
            else:
                g_out(j, j % 2).wait()
        if up:
            u_out_last().wait(); h_out_last().wait()
        else:
            g_out_last().wait()

    def down_phase(ticks):
        wd_in = pltpu.make_async_copy(WD.at[0], wd_v, wd_sem)
        wd_in.start()
        def ht_in(i, s): return pltpu.make_async_copy(HIDT.at[0, :, pl.ds(pl.multiple_of(i * TB, TB), TB)], htbuf.at[s], ht_sem.at[s])
        ht_in(0, 0).start(); x_in(0, 0).start()
        wd_in.wait()
        def step(i, carry):
            s = lax.rem(i, 2)
            for at, t in ticks.items():
                if at < nb:
                    @pl.when(i == at)
                    def _(): tick(t)
            ht_in(i, s).wait(); x_in(i, s).wait()
            @pl.when(i + 1 < nb)
            def _():
                ht_in(i + 1, 1 - s).start(); x_in(i + 1, 1 - s).start()
            @pl.when(i >= 2)
            def _():
                at_out(1, i - 2, s).wait(); h1_out(i - 2, s).wait()
            got = lax.dot_general(htbuf[s], wd_v[...], (((0,), (0,)), ((), ())), preferred_element_type=F32).astype(BF)
            h1 = (xbuf[s].astype(F32) + got.astype(F32)).astype(BF)
            h1buf[s] = h1
            h1_out(i, s).start()
            put_a(1, i, s, h1.astype(F32))
            return carry
        lax.fori_loop(0, nb, step, 0)
        for at, t in ticks.items():
            if at >= nb: tick(t)
        for i in (nb - 2, nb - 1):
            at_out(1, i, i % 2).wait(); h1_out(i, i % 2).wait()

    e7(0)
    columns_phase(WG, 0, False, {4: 5, 10: 6, 99: 7})
    e7(1)
    columns_phase(WU, 0, True, {4: 8, 10: 9, 99: 10})
    e7(2)
    down_phase({1: 11, 2: 12, 99: 13})
    e7(3)
    columns_phase(WG, 1, False, {4: 14, 10: 15, 99: 16})
    e7(4)
    columns_phase(WU, 1, True, {4: 17, 10: 18, 99: 19})
    e7(5)
    for m in range(M):
        for name in ORDER: copy(m, name).wait_send()

def fwd(n, x, wg, wu, wd):
    T, D = x.shape
    L, RG, F = wg.shape
    RD = wd.shape[1]
    rest = F % TN
    S = jax.ShapeDtypeStruct
    A = pl.BlockSpec(memory_space=pl.ANY)
    DMA = pltpu.SemaphoreType.DMA
    V = pltpu.VMEM
    return pl.pallas_call(
        functools.partial(fwd_kernel, n),
        out_shape=[S((L, D, F), BF), S((L, D, F), BF), S((L, F, D), BF), S((L, T, F), F32), S((L, T, F), F32), S((L, F, T), BF), S((L, D, T), BF), S((T, D), BF)],
        in_specs=[A] * 4, out_specs=[A] * 8,
        scratch_shapes=[
            V((T, D), BF), V((2, D, TN), BF), V((D, rest), BF), V((2, T, TN), F32), V((2, T, TN), F32), V((2, TN, T), BF),
            V((T, rest), F32), V((T, rest), F32), V((rest, T), BF), V((F, D), BF), V((2, F, TB), BF), V((2, TB, D), BF), V((2, TB, D), BF), V((2, D, TB), BF),
            V((RG, F), BF), V((RD, D), BF),
            DMA((6, 19)), DMA((6, 19)), DMA((3,)), DMA((3,)), DMA((3,)), DMA((3,)), DMA(()), DMA((2,)), DMA((2,)), DMA((2,)), DMA((2,)), DMA((6,)), DMA((6,)),
        ],
        compiler_params=pltpu.CompilerParams(collective_id=0, has_side_effects=True, vmem_limit_bytes=VMEM_LIMIT),
        name="forward",
    )(x, wg, wu, wd)


def adamw(w, m, v, g):
    m = 0.9 * m + 0.1 * g
    v = 0.95 * v + 0.05 * g * g
    step = m * lax.rsqrt(v + 1e-8) + 0.1 * w
    return (w - 0.02 * step).astype(BF), m, v


def matmul(a, b, over):
    return lax.dot_general(a, b, (((over[0],), (over[1],)), ((), ())), preferred_element_type=F32).astype(BF)


def normed(h):
    return norm_of(h.astype(F32))


def solution(mesh):
    n = mesh.shape["dp"]

    def step(x, dy, *arrays):
        weights, m, v = (arrays[i : i + 3] for i in (0, 3, 6))
        layers = weights[0].shape[0]
        h0, by_h = x[0], dy[0]
        WG, WU, WD, GATE, UP, HIDT, AT, H1 = fwd(n, h0, *weights)
        kept, mine = (h0, H1), [None] * layers
        def scattered(g):
            return lax.psum_scatter(g, "dp", scatter_dimension=0, tiled=True)
        for l in reversed(range(layers)):
            gate, up = GATE[l], UP[l]
            down = scattered(matmul(HIDT[l], by_h, (1, 0)))
            by_hid = matmul(by_h, WD[l], (1, 1)).astype(F32)
            sig = jax.nn.sigmoid(gate)
            by_up = (by_hid * gate * sig).astype(BF)
            by_gate = (by_hid * up * sig * (1 + gate * (1 - sig))).astype(BF)
            mine[l] = [scattered(matmul(AT[l], by_gate, (1, 0))), scattered(matmul(AT[l], by_up, (1, 0))), down]
            if l:
                by_a = matmul(by_gate, WG[l], (1, 1)) + matmul(by_up, WU[l], (1, 1))
                by_h = by_h + jax.vjp(normed, kept[l])[1](by_a)[0]
        gradients = [jnp.stack([mine[number][i] for number in range(layers)]).astype(F32) for i in range(3)]
        squares = lax.psum(sum(jnp.sum(g * g) for g in gradients), "dp")
        count = lax.psum(1, "dp") * sum(g.size for g in gradients)
        factor = jnp.minimum(1.0, 0.5 * lax.rsqrt(squares / count + 1e-30))
        new = [adamw(w.astype(F32), m, v, g * factor) for w, m, v, g in zip(weights, m, v, gradients, strict=True)]
        return tuple(one[which] for which in range(3) for one in new)

    states, cut = P(("rep", "dp"), None, None), P(None, "dp", None)
    return jax.shard_map(step, mesh=mesh, in_specs=(states, states) + (cut,) * 9, out_specs=(P("rep", "dp", None),) * 9, check_vma=False)
```

time: 1100 us -> 950 us (0.86)
  Pallas kernels: 0 us -> 277 us
  matrix products: 620 us -> 381 us
  waiting for transfers between devices: 349 us -> 195 us
  local copies, waits for them, and re-layouts: 30.9 us -> 2.72 us
    pallas_call x0 -> x1, Pallas kernels: none -> 277 us  [fwd(): pl.pallas_call(functools.partial(fwd_kernel, n), out_shape=[S((L, D, F),...]
    dot_general x15 -> x10, matrix products: 620 us -> 381 us  [matmul(): lax.dot_general(a, b, (((over[0],), (over[1],)), ((), ())), preferred_ele...]
    all_gather x6 -> x0, waiting for transfers between devices: 167 us -> none  [fetched(): lax.all_gather(w[number], 'dp', axis=0, tiled=True)]
    unnamed x26 -> x8, local copies, waits for them, and re-layouts: 21.1 us -> 2.72 us
    reduce_scatter x6, waiting for transfers between devices: 179 us -> 195 us  [scattered(): return lax.psum_scatter(g, 'dp', scatter_dimension=0, tiled=True)]
  transfers between devices with their start and end apart: 12 -> 6, of which waited for: 9 -> 3; matrix products, arithmetic and copies ran while one was open for 44% -> 25% of each run, Pallas kernels for 0% -> 0%
where the time goes in v1:
time: 950 us; the launch traced here: 945 us
  matrix products  381 us (40%)
  Pallas kernels  277 us (29%)
  waiting for transfers between devices  195 us (21%)
  other arithmetic  57.7 us (6%)
  between operations  17.2 us (2%)
  blocking collectives  13.3 us (1%)
    dot_general x10, matrix products, matmul(): lax.dot_general(a, b, (((over[0],), (over[1],)), ((), ())), preferred_ele...  381 us
    pallas_call x1, Pallas kernels, fwd(): pl.pallas_call(functools.partial(fwd_kernel, n), out_shape=[S((L, D, F),...  277 us
    reduce_scatter x6, waiting for transfers between devices, scattered(): return lax.psum_scatter(g, 'dp', scatter_dimension=0, tiled=True)  195 us
    convert_element_type x2, other arithmetic, adamw(): return ((w - 0.02 * step).astype(BF), m, v)  36.7 us
  transfers between devices with their start and end apart: 6, of which 3 were waited for; matrix products, arithmetic and copies ran while one was open for 25% of the time, Pallas kernels for 0%

profile of v1, /device:TPU:112, one launch (start us, length us, event | category | flops | bytes accessed | tf_op | source)
XLA Modules:
  0.0 944.7 jit_solution(13526537914171055552)
XLA Ops:
  7.2 0.1 reduce-scatter.15.cloned.1.call-start
  7.3 277.1 %forward.1 = (bf16[2,1536,4224]{2,1,0:T(8,128)(2,1)}, bf16[2,1536,4224]{2,1,0:T(8,128)(2,1)}, bf16[2,4224,1536]{2,1,0:T(8,128)(2,1)}, f32[2,2048,4224]{2,1,0:T(8...) custom-call(bf16[2048,1536]{1,0:T(8,128)(2,1)} %bitcast.141, ...), custom_call_target="tpu_custom_call" | custom-call | tf_op jit(solution)/shard_map/forward/pallas_call | solution.py:276
  284.4 51.8 %fusion.16 = (bf16[2048,4224]{1,0:T(8,128)(2,1)}, bf16[2048,4224]{1,0:T(8,128)(2,1)}) fusion(f32[2,2048,4224]{2,1,0:T(8,128)} %get-tuple-element.20, f32[2,2048,4224]{2,1,0:T(8,128)} %get-tuple-element.19, bf16[1,2048,1536]{2,1,0:T(8,128)(2,1)} %param.12, bf16[2,4224,1536]{2,1,0:T(8,128)(2,1)} %get-tuple-element.18), kind=kOutput, calls=%fused_computation.23 | convolution fusion | flops 26704871424 | bytes 123076608 | tf_op jit(solution)/shard_map/dot_general | solution.py:299
  336.2 35.7 %fusion.40 = bf16[2048,1536]{1,0:T(8,128)(2,1)} fusion(bf16[2048,4224]{1,0:T(8,128)(2,1)} %get-tuple-element.37, bf16[2,1536,4224]{2,1,0:T(8,128)(2,1)} %get-tuple-element.21), kind=kOutput, calls=%fused_computation.74 | convolution fusion | flops 26578255872 | bytes 36569088 | tf_op jit(solution)/shard_map/dot_general | solution.py:299
  371.9 37.6 %fusion.34 = (f32[2048]{0:T(1024)S(1)}, f32[2048]{0:T(1024)S(1)}, bf16[2048,1536]{1,0:T(8,128)(2,1)}) fusion(bf16[2048,1536]{1,0:T(8,128)(2,1)} %get-tuple-element.23, bf16[2048,1536]{1,0:T(8,128)(2,1)} %fusion.40, bf16[2048,4224]{1,0:T(8,128)(2,1)} %get-tuple-element.36, bf16[2,1536,4224]{2,1,0:T(8,128)(2,1)} %get-tuple-element.22), kind=kOutput, calls=%fused_computation.53 | convolution fusion | flops 26600271872 | bytes 49168384 | tf_op jit(solution)/shard_map/dot_general | solution.py:299
  409.5 8.3 fusion.64
  417.8 0.0 copy-start.3
  417.8 2.7 copy-done.3
  420.5 31.0 %convolution_convert_fusion.1 = bf16[4224,1536]{1,0:T(8,128)(2,1)} fusion(bf16[2048,1536]{1,0:T(8,128)(2,1)S(1)} %fusion.64, bf16[2,4224,2048]{2,1,0:T(8,128)(2,1)} %get-tuple-element.24), kind=kOutput, calls=%fused_computation.27 | convolution fusion | flops 26581598208 | bytes 36569088 | tf_op jit(solution)/shard_map/dot_general | solution.py:299
  451.5 0.1 reduce-scatter.15.cloned.1.call-update
  451.5 0.1 reduce-scatter.17.cloned.1.call-start
  451.6 32.8 %convolution_convert_fusion = bf16[4224,1536]{1,0:T(8,128)(2,1)} fusion(bf16[2,4224,2048]{2,1,0:T(8,128)(2,1)} %get-tuple-element.24, bf16[1,2048,1536]{2,1,0:T(8,128)(2,1)} %param.12), kind=kOutput, calls=%fused_computation.26 | convolution fusion | flops 26581598208 | bytes 36569088 | tf_op jit(solution)/shard_map/dot_general | solution.py:299
  484.5 0.1 reduce-scatter.17.cloned.1.call-update
  484.5 0.1 reduce-scatter.11.cloned.1.call-start
  484.6 36.1 %convolution_convert_fusion.6 = bf16[2048,4224]{1,0:T(8,128)(2,1)} fusion(bf16[2048,1536]{1,0:T(8,128)(2,1)} %copy-done.3, bf16[2,4224,1536]{2,1,0:T(8,128)(2,1)} %get-tuple-element.18), kind=kOutput, calls=%fused_computation.32 | convolution fusion | flops 26583760896 | bytes 36569088 | tf_op jit(solution)/shard_map/dot_general | solution.py:299
  520.7 42.5 %convolution_convert_fusion.3 = bf16[1536,4224]{1,0:T(8,128)(2,1)} fusion(bf16[2048,4224]{1,0:T(8,128)(2,1)} %convolution_convert_fusion.6, f32[2,2048,4224]{2,1,0:T(8,128)} %get-tuple-element.20, bf16[2,1536,2048]{2,1,0:T(8,128)(2,1)} %get-tuple-element.17), kind=kOutput, calls=%fused_computation.29 | convolution fusion | flops 26642153472 | bytes 71172096 | tf_op jit(solution)/shard_map/dot_general | solution.py:299
  563.1 0.1 reduce-scatter.11.cloned.1.call-update
  563.2 0.1 reduce-scatter.13.cloned.1.call-start
  563.2 35.6 %convolution_convert_fusion.2 = bf16[1536,4224]{1,0:T(8,128)(2,1)} fusion(bf16[2048,4224]{1,0:T(8,128)(2,1)} %get-tuple-element.36, bf16[2,1536,2048]{2,1,0:T(8,128)(2,1)} %get-tuple-element.17), kind=kOutput, calls=%fused_computation.28 | convolution fusion | flops 26581598208 | bytes 36569088 | tf_op jit(solution)/shard_map/dot_general | solution.py:299
  598.8 0.1 reduce-scatter.13.cloned.1.call-update
  598.9 0.1 reduce-scatter.7.cloned.1.call-start
  598.9 42.8 %convolution_convert_fusion.5 = bf16[1536,4224]{1,0:T(8,128)(2,1)} fusion(bf16[2048,4224]{1,0:T(8,128)(2,1)} %convolution_convert_fusion.6, f32[2,2048,4224]{2,1,0:T(8,128)} %get-tuple-element.19, f32[2,2048,4224]{2,1,0:T(8,128)} %get-tuple-element.20, bf16[2,1536,2048]{2,1,0:T(8,128)(2,1)} %get-tuple-element.17), kind=kOutput, calls=%fused_computation.31 | convolution fusion | flops 26676756480 | bytes 105775104 | tf_op jit(solution)/shard_map/dot_general | solution.py:299
  641.7 0.1 reduce-scatter.7.cloned.1.call-update
  641.8 0.1 reduce-scatter.9.cloned.1.call-start
  641.9 35.6 %convolution_convert_fusion.4 = bf16[1536,4224]{1,0:T(8,128)(2,1)} fusion(bf16[2048,4224]{1,0:T(8,128)(2,1)} %get-tuple-element.37, bf16[2,1536,2048]{2,1,0:T(8,128)(2,1)} %get-tuple-element.17), kind=kOutput, calls=%fused_computation.30 | convolution fusion | flops 26581598208 | bytes 36569088 | tf_op jit(solution)/shard_map/dot_general | solution.py:299
  677.5 0.1 reduce-scatter.9.cloned.1.call-update
  677.5 0.0 copy-start.2
  677.5 0.0 reduce-scatter.15.cloned.1.call-done
  677.6 0.0 reduce-scatter.17.cloned.1.call-done
  677.6 4.3 fusion.54
  681.9 0.0 reduce-scatter.11.cloned.1.call-done
  681.9 54.5 %reduce-scatter.13.cloned.1.call-done = bf16[192,4224]{1,0:T(8,128)(2,1)} async-done(((bf16[1536,4224]{1,0:T(8,128)(2,1)}), bf16[192,4224]{1,0:T(8,128)(2,1)}) %reduce-scatter.13.cloned.1.call-update) | async-done | bytes 1622032 | tf_op jit(solution)/shard_map/reduce_scatter | solution.py:316
  736.5 4.2 fusion.53
  740.6 67.9 %reduce-scatter.7.cloned.1.call-done = bf16[192,4224]{1,0:T(8,128)(2,1)} async-done(((bf16[1536,4224]{1,0:T(8,128)(2,1)}), bf16[192,4224]{1,0:T(8,128)(2,1)}) %reduce-scatter.7.cloned.1.call-update) | async-done | bytes 1622032 | tf_op jit(solution)/shard_map/reduce_scatter | solution.py:316
  808.5 72.1 %reduce-scatter.9.cloned.1.call-done = bf16[192,4224]{1,0:T(8,128)(2,1)} async-done(((bf16[1536,4224]{1,0:T(8,128)(2,1)}), bf16[192,4224]{1,0:T(8,128)(2,1)}) %reduce-scatter.9.cloned.1.call-update) | async-done | bytes 1622032 | tf_op jit(solution)/shard_map/reduce_scatter | solution.py:316
  880.7 4.2 fusion.52
  886.8 13.3 %psum.7 = f32[]{:T(128)} all-reduce(f32[]{:T(128)S(6)} %add.102), channel_id=1, replica_groups=mesh['rep'=2,'dp'=8] {'dp'}, use_global_device_ids=true, to_apply=%region_11.0 | all-reduce | flops 1 | bytes 8 | tf_op jit(solution)/shard_map/psum | solution.py:329
  900.8 0.0 copy-done.2
  900.8 0.0 copy-start
  900.8 0.0 copy-start.1
  900.8 11.9 %fusion.60 = (bf16[2,528,1536]{2,1,0:T(8,128)(2,1)}, f32[2,528,1536]{2,1,0:T(8,128)}, f32[2,528,1536]{2,1,0:T(8,128)}) fusion(bf16[2,528,1536]{2,1,0:T(8,128)(2,1)S(1)} %copy-done.2, f32[]{:T(128)S(6)} %min.3, bf16[1,528,1536]{2,1,0:T(8,128)(2,1)} %bitcast.132, bf16[1,528,1536]{2,1,0:T(8,128)(2,1)} %bitcast.130, f32[2,528,1536]{2,1,0:T(8,128)} %param.21, ...), kind=kLoop, calls=%fused_computation.90 | loop fusion | flops 32440320 | bytes 35684356 | tf_op jit(solution)/shard_map/convert_element_type | solution.py:295
  912.7 0.0 copy-done
  912.7 0.0 copy-done.1
  912.7 24.8 %fusion.51 = (bf16[2,192,4224]{2,1,0:T(8,128)(2,1)}, f32[2,192,4224]{2,1,0:T(8,128)}, f32[2,192,4224]{2,1,0:T(8,128)}, bf16[2,192,4224]{2,1,0:T(8,128)(2,1)}, f3...) fusion(bf16[2,192,4224]{2,1,0:T(8,128)(2,1)S(1)} %copy-done, f32[]{:T(128)S(6)} %min.3, ...), kind=kLoop, calls=%fused_computation.81 | loop fusion | flops 64880640 | bytes 71368704 | tf_op jit(solution)/shard_map/convert_element_type | solution.py:295
  (1 shorter events, 0.0 us)
Async XLA Ops:
  7.2 670.4 %reduce-scatter.15.cloned.1.call-start = ((), (), s32[]{:S(2)}) async-start(), calls=%async_computation.10 | async-start | bytes 14598144 | tf_op jit(solution)/shard_map/reduce_scatter | solution.py:316
  417.8 2.7 copy-start.3
  451.5 226.0 %reduce-scatter.17.cloned.1.call-start = ((), (), s32[]{:S(2)}) async-start(), calls=%async_computation.11 | async-start | bytes 14598144 | tf_op jit(solution)/shard_map/reduce_scatter | solution.py:316
  484.5 197.4 %reduce-scatter.11.cloned.1.call-start = ((), (), s32[]{:S(2)}) async-start(), calls=%async_computation.8 | async-start | bytes 14598144 | tf_op jit(solution)/shard_map/reduce_scatter | solution.py:316
  563.2 173.3 %reduce-scatter.13.cloned.1.call-start = ((), (), s32[]{:S(2)}) async-start(), calls=%async_computation.9 | async-start | bytes 14598144 | tf_op jit(solution)/shard_map/reduce_scatter | solution.py:316
  598.9 209.7 %reduce-scatter.7.cloned.1.call-start = ((), (), s32[]{:S(2)}) async-start(), calls=%async_computation.6 | async-start | bytes 14598144 | tf_op jit(solution)/shard_map/reduce_scatter | solution.py:316
  641.8 238.8 %reduce-scatter.9.cloned.1.call-start = ((), (), s32[]{:S(2)}) async-start(), calls=%async_computation.7 | async-start | bytes 14598144 | tf_op jit(solution)/shard_map/reduce_scatter | solution.py:316
  677.5 223.3 %copy-start.2 = (bf16[2,528,1536]{2,1,0:T(8,128)(2,1)S(1)}, bf16[2,528,1536]{2,1,0:T(8,128)(2,1)}, u32[]{:S(2)}) copy-start(bf16[2,528,1536]{2,1,0:T(8,128)(2,1)} %wd.1) | copy-start | bytes 9732100
  900.8 11.9 %copy-start = (bf16[2,192,4224]{2,1,0:T(8,128)(2,1)S(1)}, bf16[2,192,4224]{2,1,0:T(8,128)(2,1)}, u32[]{:S(2)}) copy-start(bf16[2,192,4224]{2,1,0:T(8,128)(2,1)} %wg.1) | copy-start | bytes 9732100
  900.8 11.9 %copy-start.1 = (bf16[2,192,4224]{2,1,0:T(8,128)(2,1)S(1)}, bf16[2,192,4224]{2,1,0:T(8,128)(2,1)}, u32[]{:S(2)}) copy-start(bf16[2,192,4224]{2,1,0:T(8,128)(2,1)} %wu.1) | copy-start | bytes 9732100
Sparse Core Ops, SparseCore 0:
  451.7 68.1 reduce-scatter.14
  522.2 69.8 reduce-scatter.16
  594.4 69.8 reduce-scatter.10
  666.5 69.8 reduce-scatter.12
  738.6 69.8 reduce-scatter.6
  810.7 69.8 reduce-scatter.8

commit v2 on v0

v2 whole, which is shorter than its diff:
```python
import functools
import jax, jax.numpy as jnp
from jax import lax
from jax.experimental import pallas as pl
from jax.experimental.pallas import tpu as pltpu
from jax.sharding import PartitionSpec as P
ZERO, ONE, TWO = range(3)
MESH=pl.DeviceIdType.MESH
BF, F32 = jnp.bfloat16, jnp.float32
VMEM_LIMIT = 67043328

def norm_of(wide):
    return (wide * lax.rsqrt(jnp.mean(wide * wide, -ONE, keepdims=True) + 1e-6)).astype(BF)

TN = 256
TD = 256
TB = 512
CH = 512

def fwd_kernel(n, x, wg, wu, wd, WG, WU, WD, GATE, UP, HIDT, AT, H1, WGT, WUT,
               a_v, xbuf, atbuf,
               send, recv, w_sem, g_sem, go_sem, u_sem, h_sem, t_sem, wd_sem, ht_sem, x_sem, h1_sem, at_sem, b_sem, b_out):
    T, D = x.shape
    F = wg.shape[TWO]
    full = F // TN
    rest = F - full * TN
    r, me = lax.axis_index("rep"), lax.axis_index("dp")
    right, left = lax.rem(me + TWO, n), lax.rem(me + n - TWO, n)
    across = lax.rem(me + n // TWO, n)
    odd = lax.rem(me, TWO)
    sib = me + ONE - TWO * odd
    par = lax.rem(r, TWO)
    partner = r + ONE - TWO * par
    to = {"R": (r, right), "L": (r, left), "S": (r, sib), "Y": (partner, me)}

    def twin(d):
        return d + ONE - TWO * odd

    shards = [(wg, WG, ZERO), (wu, WU, ZERO), (wd, WD, ZERO), (wg, WG, ONE), (wu, WU, ONE), (wd, WD, ONE)]

    def moves(m):
        w, W, l = shards[m]
        R = w.shape[ONE]
        c = R // 3
        N, P1, P2, ALL = (ZERO, c), (c * (ONE + par), c), (c * (TWO - par), c), (ZERO, R)
        return {
            "rN": (me, N, "R", True), "lP": (me, P1, "L", True), "rP": (me, P1, "R", True), "lN": (me, N, "L", True),
            "sO": (me, ALL, "S", True),
            "oN": (left, N, "R", False), "oP": (right, P1, "L", False),
            "ylP": (right, P1, "Y", False), "yrP": (left, P1, "Y", False), "yoP": (across, P1, "Y", False),
            "srN": (left, N, "S", False), "srP": (left, P1, "S", False), "slP": (right, P1, "S", False), "slN": (right, N, "S", False),
            "soN": (across, N, "S", False), "soP": (across, P1, "S", False),
            "syl": (right, P2, "S", False), "syr": (left, P2, "S", False), "syo": (across, P2, "S", False),
        }

    ORDER = list(moves(ZERO))

    def copy(m, name):
        w, W, l = shards[m]
        R = w.shape[ONE]
        owner, (first, rows), way, own = moves(m)[name]
        there = W.at[l, pl.ds(pl.multiple_of(owner * R + first, 8), rows)]
        src = w.at[l, pl.ds(pl.multiple_of(first, 8) if not isinstance(first, int) else first, rows)] if own else there
        k = ORDER.index(name)
        return pltpu.make_async_remote_copy(src_ref=src, dst_ref=there, send_sem=send.at[m, k], recv_sem=recv.at[m, k],
                                            device_id=to[way], device_id_type=MESH)

    def start(m, *names):
        for name in names:
            copy(m, name).start()

    def arrive(m, *names):
        for name in names:
            copy(m, name).wait_recv()

    def e1(m): start(m, "rN", "lP", "rP", "lN", "sO")
    def e2(m):
        arrive(m, "rN", "lP"); start(m, "oN", "oP", "ylP", "srN", "slP")
    def e3(m):
        arrive(m, "rP", "lN"); start(m, "yrP", "srP", "slN")
    def e4(m):
        arrive(m, "oN", "oP", "ylP"); start(m, "yoP", "soN", "soP", "syl")
    def e5(m):
        arrive(m, "yrP"); start(m, "syr")
    def e6(m):
        arrive(m, "yoP"); start(m, "syo")
    def e7(m):
        arrive(m, "sO", "srN", "srP", "slP", "slN", "soN", "soP", "syl", "syr", "syo")

    M = len(shards)
    def tick(t):
        m, phase = divmod(t, 3)
        if phase == ZERO:
            if ZERO <= m - ONE < M: e4(m - ONE); e5(m - ONE)
        elif phase == ONE:
            if m < M: e2(m)
            if ZERO <= m - ONE < M: e6(m - ONE)
        else:
            if m < M: e3(m)
            if m + ONE < M: e1(m + ONE)

    barrier = pltpu.get_barrier_semaphore()
    for way in to:
        pl.semaphore_signal(barrier, inc=ONE, device_id=to[way], device_id_type=MESH)
    pl.semaphore_wait(barrier, 4)
    e1(ZERO)

    nb = T // TB
    def x_in(i, s): return pltpu.make_async_copy(x.at[pl.ds(i * TB, TB)], xbuf.at[s], x_sem.at[s])
    def at_out(l, i, s): return pltpu.make_async_copy(atbuf.at[s], AT.at[l, :, pl.ds(i * TB, TB)], at_sem.at[s])
    def put_a(l, i, s, wide):
        a = norm_of(wide)
        a_v[pl.ds(i * TB, TB)] = a
        atbuf[s] = a.T
        at_out(l, i, s).start()
    def settle_own(bounce, bounced):
        def slot_of(m):
            return bounced if shards[m][ZERO] is wd else bounce
        def own_in(m):
            w, W, l = shards[m]
            return pltpu.make_async_copy(w.at[l], slot_of(m), b_sem.at[m])
        def own_out(m):
            w, W, l = shards[m]
            R = w.shape[ONE]
            return pltpu.make_async_copy(slot_of(m), W.at[l, pl.ds(pl.multiple_of(me * R, 8), R)], b_out.at[m])
        own_in(ZERO).start(); own_in(TWO).start()
        x_in(ZERO, ZERO).start()
        for i in range(nb):
            s = i % TWO
            x_in(i, s).wait()
            if i + ONE < nb: x_in(i + ONE, ONE - s).start()
            if i >= TWO: at_out(ZERO, i - TWO, s).wait()
            put_a(ZERO, i, s, xbuf[s].astype(F32))
        for i in (nb - TWO, nb - ONE): at_out(ZERO, i, i % TWO).wait()
        own_in(TWO).wait(); own_out(TWO).start()
        for m, after in ((ZERO, ONE), (ONE, 3), (3, 4), (4, None)):
            own_in(m).wait(); own_out(m).start(); own_out(m).wait()
            if after is not None: own_in(after).start()
            if m == ZERO:
                own_out(TWO).wait(); own_in(5).start()
        own_in(5).wait(); own_out(5).start(); own_out(5).wait()
    pl.run_scoped(settle_own, pltpu.VMEM(wg.shape[ONE:], BF), pltpu.VMEM(wd.shape[ONE:], BF))

    for t in (ONE, TWO, 3, 4): tick(t)

    def cols(j): return pl.ds(pl.multiple_of(j * TN, TN), TN)
    LAST = pl.ds(full * TN, rest)

    def columns_phase(W, WT, l, up, ticks):
        turn = WT is not None
        def body(wbuf, gbuf, ubuf, hbuf, tbuf, wtail, gtail, utail, htail, ttail):
            LASTC = (full, slice(None), pl.ds(ZERO, rest))
            def ins(j, s):
                got = [pltpu.make_async_copy(W.at[l, :, cols(j)], wbuf.at[s], w_sem.at[s])]
                if up: got.append(pltpu.make_async_copy(GATE.at[l, j], gbuf.at[s], g_sem.at[s]))
                return got
            def ins_last():
                got = [pltpu.make_async_copy(W.at[l, :, LAST], wtail, w_sem.at[3])]
                if up: got.append(pltpu.make_async_copy(GATE.at[l, full, :, pl.ds(ZERO, rest)], gtail, g_sem.at[3]))
                return got
            def outs(j, s):
                if up:
                    got = [pltpu.make_async_copy(ubuf.at[s], UP.at[l, j], u_sem.at[s]), pltpu.make_async_copy(hbuf.at[s], HIDT.at[l, cols(j)], h_sem.at[s])]
                else:
                    got = [pltpu.make_async_copy(gbuf.at[s], GATE.at[l, j], go_sem.at[s])]
                if turn: got.append(pltpu.make_async_copy(tbuf.at[s], WT.at[:, cols(j)], t_sem.at[s]))
                return got
            def outs_last():
                if up:
                    got = [pltpu.make_async_copy(utail, UP.at[l, full, :, pl.ds(ZERO, rest)], u_sem.at[TWO]), pltpu.make_async_copy(htail, HIDT.at[l, LAST], h_sem.at[TWO])]
                else:
                    got = [pltpu.make_async_copy(gtail, GATE.at[l, full, :, pl.ds(ZERO, rest)], go_sem.at[TWO])]
                if turn: got.append(pltpu.make_async_copy(ttail, WT.at[:, LAST], t_sem.at[TWO]))
                return got
            def compute(w_ref, g_ref, u_ref, h_ref, t_ref):
                for c in range(T // CH):
                    rows = pl.ds(c * CH, CH)
                    got = jnp.dot(a_v[rows], w_ref[...], preferred_element_type=F32)
                    if not up:
                        g_ref[rows] = got
                    else:
                        g = g_ref[rows]
                        u_ref[rows] = got
                        hid = (g * (ONE / (ONE + jnp.exp(-g))) * got).astype(BF)
                        h_ref[:, rows] = hid.T
                if turn:
                    for d in range(D // TD):
                        t_ref[d] = w_ref[d * TD:(d + ONE) * TD].T
            for j in (ZERO, ONE):
                for c in ins(j, j): c.start()
            def step(j, carry):
                s, o = lax.rem(j, 3), lax.rem(j, TWO)
                for at, t in ticks.items():
                    if at < full:
                        @pl.when(j == at)
                        def _(): tick(t)
                for c in ins(j, s): c.wait()
                @pl.when(j + TWO < full)
                def _():
                    for c in ins(j + TWO, lax.rem(j + TWO, 3)): c.start()
                @pl.when(j + TWO == full)
                def _():
                    for c in ins_last(): c.start()
                @pl.when(j >= TWO)
                def _():
                    for c in outs(j - TWO, o): c.wait()
                compute(wbuf.at[s], gbuf.at[s] if up else gbuf.at[o], ubuf.at[o], hbuf.at[o], tbuf.at[o])
                for c in outs(j, o): c.start()
                return carry
            lax.fori_loop(ZERO, full, step, ZERO)
            for c in ins_last(): c.wait()
            compute(wtail, gtail, utail, htail, ttail)
            for c in outs_last(): c.start()
            for at, t in ticks.items():
                if at >= full: tick(t)
            for j in (full - TWO, full - ONE):
                for c in outs(j, j % TWO): c.wait()
            for c in outs_last(): c.wait()
        V = pltpu.VMEM
        nd = D // TD
        pl.run_scoped(body, V((3, D, TN), BF), V((3, T, TN), F32), V((TWO, T, TN) if up else (TWO, 8, 128), F32), V((TWO, TN, T) if up else (TWO, 8, 128), BF),
                      V((TWO, nd, TN, TD) if turn else (TWO, 8, 128), BF), V((D, rest), BF), V((T, rest), F32), V((T, rest), F32), V((rest, T), BF), V((nd, rest, TD), BF))

    def down_phase(ticks):
        def body(wd_v, htbuf, h1buf):
            def h1_out(i, s): return pltpu.make_async_copy(h1buf.at[s], H1.at[pl.ds(i * TB, TB)], h1_sem.at[s])
            wd_in = pltpu.make_async_copy(WD.at[ZERO], wd_v, wd_sem)
            wd_in.start()
            def ht_in(i, s): return pltpu.make_async_copy(HIDT.at[ZERO, :, pl.ds(pl.multiple_of(i * TB, TB), TB)], htbuf.at[s], ht_sem.at[s])
            ht_in(ZERO, ZERO).start(); x_in(ZERO, ZERO).start()
            wd_in.wait()
            def step(i, carry):
                s = lax.rem(i, TWO)
                for at, t in ticks.items():
                    if at < nb:
                        @pl.when(i == at)
                        def _(): tick(t)
                ht_in(i, s).wait(); x_in(i, s).wait()
                @pl.when(i + ONE < nb)
                def _():
                    ht_in(i + ONE, ONE - s).start(); x_in(i + ONE, ONE - s).start()
                @pl.when(i >= TWO)
                def _():
                    at_out(ONE, i - TWO, s).wait(); h1_out(i - TWO, s).wait()
                got = lax.dot_general(htbuf[s], wd_v[...], (((ZERO,), (ZERO,)), ((), ())), preferred_element_type=F32).astype(BF)
                h1 = (xbuf[s].astype(F32) + got.astype(F32)).astype(BF)
                h1buf[s] = h1
                h1_out(i, s).start()
                put_a(ONE, i, s, h1.astype(F32))
                return carry
            lax.fori_loop(ZERO, nb, step, ZERO)
            for at, t in ticks.items():
                if at >= nb: tick(t)
            for i in (nb - TWO, nb - ONE):
                at_out(ONE, i, i % TWO).wait(); h1_out(i, i % TWO).wait()
        pl.run_scoped(body, pltpu.VMEM((F, D), BF), pltpu.VMEM((TWO, F, TB), BF), pltpu.VMEM((TWO, TB, D), BF))

    e7(ZERO)
    columns_phase(WG, None, ZERO, False, {4: 5, 10: 6, 99: 7})
    e7(ONE)
    columns_phase(WU, None, ZERO, True, {4: 8, 10: 9, 99: 10})
    e7(TWO)
    down_phase({ONE: 11, TWO: 12, 99: 13})
    e7(3)
    columns_phase(WG, WGT, ONE, False, {4: 14, 10: 15, 99: 16})
    e7(4)
    columns_phase(WU, WUT, ONE, True, {4: 17, 10: 18, 99: 19})
    e7(5)
    for m in range(M):
        for name in ORDER: copy(m, name).wait_send()

def fwd(n, x, wg, wu, wd):
    T, D = x.shape
    L, RG, F = wg.shape
    RD = wd.shape[ONE]
    steps = pl.cdiv(F, TN)
    S = jax.ShapeDtypeStruct
    A = pl.BlockSpec(memory_space=pl.ANY)
    DMA = pltpu.SemaphoreType.DMA
    V = pltpu.VMEM
    return pl.pallas_call(
        functools.partial(fwd_kernel, n),
        out_shape=[S((L, D, F), BF), S((L, D, F), BF), S((L, F, D), BF), S((L, steps, T, TN), F32), S((L, steps, T, TN), F32), S((L, F, T), BF), S((L, D, T), BF), S((T, D), BF),
                   S((D // TD, F, TD), BF), S((D // TD, F, TD), BF)],
        in_specs=[A] * 4, out_specs=[A] * 10,
        scratch_shapes=[
            V((T, D), BF), V((TWO, TB, D), BF), V((TWO, D, TB), BF),
            DMA((6, 19)), DMA((6, 19)), DMA((4,)), DMA((4,)), DMA((3,)), DMA((3,)), DMA((3,)), DMA((3,)), DMA(()), DMA((TWO,)), DMA((TWO,)), DMA((TWO,)), DMA((TWO,)), DMA((6,)), DMA((6,)),
        ],
        compiler_params=pltpu.CompilerParams(collective_id=ZERO, has_side_effects=True, vmem_limit_bytes=VMEM_LIMIT),
        name="forward",
    )(x, wg, wu, wd)


class Chunk:
    def __init__(self, kind, mi, first, width, number):
        self.kind, self.mi, self.first, self.width, self.number = kind, mi, first, width, number


def planned(phases, chunks, ready):
    now, plan, tail = 0.0, {}, []
    free = {"S": 0.0, "R": 0.0, "L": 0.0}
    sets = {"g": [ZERO, ONE], "d": [ZERO]}
    state = {q: ["S0", None] for q in chunks}
    order = ["S0", "L1", "C1", "L2", "C2", "L3", "C3", "L4", "C4", "end"]
    load = 1.8

    def send(way, size, rate):
        free[way] = max(free[way], now) + size / rate
        return free[way] + 2.0

    def run(point):
        done = []
        again = True
        while again:
            again = False
            for q in chunks:
                stage, when = state[q]
                if stage == "end":
                    continue
                size = q.rows * q.width * TWO
                if stage == "S0":
                    if point is not None and point < ready[q]:
                        continue
                    if q.kind == "g":
                        done.append(("S0", q, ZERO))
                        state[q] = ["L1", send("S", 4 * size, 6e5)]
                    else:
                        state[q] = ["L1", now + 5]
                    again = True
                    continue
                if when > now:
                    continue
                if stage[ZERO] == "L":
                    if not sets[q.kind]:
                        continue
                    q.set = sets[q.kind].pop(ZERO)
                    done.append((stage, q, q.set))
                    state[q] = ["C" + stage[ONE], now + load]
                    again = True
                    continue
                sets[q.kind].append(q.set)
                done.append((stage, q, q.set))
                nxt = order[order.index(stage) + ONE]
                if stage == "C1":
                    when = max(send("R", size / TWO, 46600), send("L", size / TWO, 46600))
                elif stage == "C2":
                    q.right = send("R", size, 46600)
                    when = now
                elif stage == "C3":
                    when = max(q.right, send("L", size, 46600))
                state[q] = [nxt, when]
                again = True
        return done

    for p, (name, points, us) in enumerate(phases):
        for s in range(points):
            got = run((p, s))
            if got:
                plan[name, s] = got
            now += us + 0.3 * len(got)
    last = now
    while any(state[q][ZERO] != "end" for q in chunks):
        got = run(None)
        tail += got
        now += 0.5 + 0.3 * len(got)
    return plan, tail, last, now


CUTS = (5, 10, 14)


def bwd_kernel(n, dy, H1, WGT, WUT, WD, GATE, UP, HIDT, AT,
               GG, GU, GD, SQ, DG, DU, OWNg, Tg, ARg, X1g, X2g, OWNd, Td, ARd, X1d, X2d,
               dyv, sqv, og, ag, xg, yg, o1g, o2g, o3g, o4g, od, ad, xd, yd, o1d, o2d, o3d, o4d,
               slots, s0s, s0r, d0s, d0r, x1s, x1r, x2s, x2r, ld, fin, sems, one, ts, tr):
    T, D = dy.shape
    L, F, _ = WD.shape
    chips = n // TWO
    RG, RD = D // n, F // n
    full, rest = F // TN, F % TN
    r, me = lax.axis_index("rep"), lax.axis_index("dp")
    right, left = lax.rem(me + TWO, n), lax.rem(me + n - TWO, n)
    core = lax.rem(me, TWO)
    chip = lax.div(me, TWO)
    sib = me + ONE - TWO * core
    to = {"R": (r, right), "L": (r, left), "S": (r, sib)}
    at_chip = [lax.rem(chip + k, chips) for k in range(chips)]
    FAR = (chips // TWO, ONE, chips - ONE, ZERO)

    DI, GI = {"d1": ZERO, "d0": ONE}, {"g1": ZERO, "u1": ONE, "g0": TWO, "u0": 3}
    edges = [ZERO] + [k * TN for k in CUTS] + [F]
    last_step = [k - ONE for k in CUTS] + [full]
    chunks = []
    for pair in (("d1",), ("g1", "u1"), ("d0",), ("g0", "u0")):
        for c in range(TWO if pair[ZERO] in DI else len(edges) - ONE):
            for nm in pair:
                down = nm in DI
                a, w = (c * (D // TWO), D // TWO) if down else (edges[c], edges[c + ONE] - edges[c])
                q = Chunk("d" if down else "g", DI.get(nm, GI.get(nm)), a, w, c)
                q.rows, q.name = (RD if down else RG), nm
                q.half = (q.rows // 32 * 16, q.rows - q.rows // 32 * 16)
                chunks.append(q)
    nt = T // TB
    phases = [("d1", chips, 8.3), ("m1", TWO * full + TWO, 2.7), ("a1", nt * (D // TD), 3.4), ("d0", chips, 8.3), ("m0", TWO * full + TWO, 2.7)]
    index = {p[ZERO]: i for i, p in enumerate(phases)}
    ready = {}
    for q in chunks:
        if q.kind == "d":
            ready[q] = (index[q.name], TWO)
        elif last_step[q.number] == full:
            ready[q] = (index["m" + q.name[ONE]] + ONE, ZERO)
        else:
            ready[q] = (index["m" + q.name[ONE]], TWO * (last_step[q.number] + ONE) + ONE)
    plan, tail, _, _ = planned(phases, chunks, ready)

    refs = {"g": (OWNg, Tg, ARg, X1g, X2g, og, ag, xg, yg, (o1g, o2g, o3g, o4g)),
            "d": (OWNd, Td, ARd, X1d, X2d, od, ad, xd, yd, (o1d, o2d, o3d, o4d))}
    outs = {"g1": (GG, ONE), "u1": (GU, ONE), "d1": (GD, ONE), "g0": (GG, ZERO), "u0": (GU, ZERO), "d0": (GD, ZERO)}
    def remote(src, dst, ss, rs, way):
        return pltpu.make_async_remote_copy(src_ref=src, dst_ref=dst, send_sem=ss, recv_sem=rs, device_id=to[way], device_id_type=MESH)

    sent = []

    def cols_of(q): return pl.ds(q.first, q.width)

    def s0_copy(q):
        return remote(Tg.at[q.mi, :, :, cols_of(q)], ARg.at[q.mi, :, :, cols_of(q)], s0s.at[q.mi, q.number], s0r.at[q.mi, q.number], "S")

    def d0_copy(mi, i, where):
        return remote(Td.at[mi, where], ARd.at[mi, where], d0s.at[mi, i], d0r.at[mi, i], "S")

    def sem_of(q): return (q.mi if q.kind == "g" else 4 + q.mi), q.number

    slot, before, user = {}, {}, {}
    in_order = [e for name, points, _ in phases for s in range(points) for e in plan.get((name, s), ())] + tail
    for kind, q, _ in in_order:
        if kind[ZERO] == "C":
            key = (q.kind, int(kind[ONE]))
            k = len([p for p in slot if p[ONE] == key[ONE] and p[ZERO].kind == q.kind]) % refs[q.kind][9][ZERO].shape[ZERO]
            slot[q, key[ONE]], before[q, key[ONE]] = k, user.get(key + (k,))
            user[key + (k,)] = q

    def out_of(q, stage):
        return refs[q.kind][9][stage - ONE].at[slot[q, stage]]

    def result_copy(q):
        G, l = outs[q.name]
        k = slot[q, 4]
        return pltpu.make_async_copy(out_of(q, 4).at[:, pl.ds(ZERO, q.width)], G.at[l, :, cols_of(q)], fin.at[k if q.kind == "g" else TWO])

    def settle(q, stage):
        if q is None: return
        if stage == ONE:
            for half in (ZERO, ONE): x1_copy(q, half).wait_send()
        elif stage < 4:
            x2_copy(q, stage - TWO).wait_send()
        else:
            result_copy(q).wait()

    def x1_copy(q, half):
        X1, out = refs[q.kind][3], out_of(q, ONE)
        h = pl.ds(ZERO, q.half[half])
        a, c = sem_of(q)
        return remote(out.at[pl.ds(half * q.half[ZERO], q.half[half]), pl.ds(ZERO, q.width)], X1.at[q.mi, half, h, cols_of(q)], x1s.at[a, c, half], x1r.at[a, c, half], "RL"[half])

    def x2_copy(q, side):
        X2, out = refs[q.kind][4], out_of(q, TWO + side)
        a, c = sem_of(q)
        return remote(out.at[:, pl.ds(ZERO, q.width)], X2.at[q.mi, side, :, cols_of(q)], x2s.at[a, c, side], x2r.at[a, c, side], "RL"[side])

    def loads(stage, q, z):
        OWN, _, AR, X1, X2, vo, va, vx, vy, _ = refs[q.kind]
        vo, va, vx, vy = vo.at[z], va.at[z], vx.at[z], vy.at[z]
        where = at_chip[FAR[stage - ONE]]
        base = 4 * z if q.kind == "g" else 8
        h = q.half
        w = pl.ds(ZERO, q.width)
        got = [pltpu.make_async_copy(OWN.at[q.mi, where, :, cols_of(q)], vo.at[:, w], ld.at[base]),
               pltpu.make_async_copy(AR.at[q.mi, where, :, cols_of(q)], va.at[:, w], ld.at[base + ONE])]
        if stage == TWO:
            got.append(pltpu.make_async_copy(X1.at[q.mi, ZERO, pl.ds(ZERO, h[ZERO]), cols_of(q)], vx.at[pl.ds(ZERO, h[ZERO]), w], ld.at[base + TWO]))
        if stage == 3:
            got.append(pltpu.make_async_copy(X1.at[q.mi, ONE, pl.ds(ZERO, h[ONE]), cols_of(q)], vx.at[pl.ds(h[ZERO], h[ONE]), w], ld.at[base + TWO]))
        if stage == 4:
            got.append(pltpu.make_async_copy(X2.at[q.mi, ZERO, :, cols_of(q)], vx.at[:, w], ld.at[base + TWO]))
            got.append(pltpu.make_async_copy(X2.at[q.mi, ONE, :, cols_of(q)], vy.at[:, w], ld.at[base + 3]))
        return got

    STEP = {"g": 48, "d": 16}

    def event(kind, q, z):
        stage = int(kind[ONE])
        if kind == "S0":
            s0_copy(q).start()
            sent.append(lambda: s0_copy(q).wait_send())
            return
        vo, va, vx, vy = refs[q.kind][5:9]
        if kind[ZERO] == "L":
            if q.kind == "g":
                if stage == ONE: s0_copy(q).wait_recv()
            elif q.number == ZERO:
                d0_copy(q.mi, stage - ONE, at_chip[FAR[stage - ONE]]).wait_recv()
            if stage == TWO: x1_copy(q, ZERO).wait_recv()
            if stage == 3: x1_copy(q, ONE).wait_recv()
            if stage == 4:
                x2_copy(q, ZERO).wait_recv(); x2_copy(q, ONE).wait_recv()
            for c in loads(stage, q, z): c.start()
            return
        for c in loads(stage, q, z): c.wait()
        out, k = refs[q.kind][9][stage - ONE], slot[q, stage]
        settle(before[q, stage], stage)
        w, h = pl.ds(ZERO, q.width), q.half[ZERO]
        by = STEP[q.kind]

        def rows_loop(first, count, fn):
            def body(i, carry):
                fn(pl.ds(pl.multiple_of(first + i * by, 16), by))
                return carry
            lax.fori_loop(ZERO, count // by, body, ZERO)

        def plain(rows):
            out[k, rows, w] = (vo[z, rows, w] + va[z, rows, w].astype(F32)).astype(BF)
        def one_more(rows):
            out[k, rows, w] = (vo[z, rows, w] + va[z, rows, w].astype(F32) + vx[z, rows, w].astype(F32)).astype(BF)
        def final(rows):
            g = (vo[z, rows, w] + va[z, rows, w].astype(F32) + vx[z, rows, w].astype(F32) + vy[z, rows, w].astype(F32)).astype(BF)
            out[k, rows, w] = g
            g = g.astype(F32)
            g = g * g
            total = g[ZERO:8]
            for p in range(8, by, 8): total = total + g[p:p + 8]
            sqv[:, w] += total
        if stage == ONE:
            rows_loop(ZERO, q.rows, plain)
            for half in (ZERO, ONE): x1_copy(q, half).start()
        elif stage in (TWO, 3):
            rows_loop(ZERO, h, one_more if stage == TWO else plain); rows_loop(h, q.half[ONE], plain if stage == TWO else one_more)
            x2_copy(q, stage - TWO).start()
        else:
            rows_loop(ZERO, q.rows, final)
            result_copy(q).start()

    def events(name, j, steps, parity=None):
        for s in range(steps):
            if (name, s) in plan and parity in (None, s % TWO):
                @pl.when(j == s)
                def _():
                    for e in plan[name, s]: event(*e)

    def events_at(name, s):
        for e in plan.get((name, s), ()): event(*e)

    others = [lax.rem(me + k, n) for k in range(ONE, n)]
    barrier = pltpu.get_barrier_semaphore()
    for other in others:
        pl.semaphore_signal(barrier, inc=ONE, device_id=(r, other), device_id_type=MESH)
    pl.semaphore_wait(barrier, n - ONE)
    first = pltpu.make_async_copy(dy, dyv, one)
    first.start()
    sqv[...] = jnp.zeros_like(sqv)
    first.wait()

    def cols(j): return pl.ds(pl.multiple_of(j * TN, TN), TN)
    LAST = pl.ds(full * TN, rest)

    def far(i):
        k = jnp.where(i == ZERO, FAR[ZERO], jnp.where(i == ONE, FAR[ONE], jnp.where(i == TWO, FAR[TWO], FAR[3])))
        return lax.rem(chip + k, chips)

    def down_weights(name, l):
        mi = DI[name]
        def body(lhs, mb, tb):
            def rows(i, w): return pl.ds(pl.multiple_of((TWO * far(i) + (ONE - core if w == ZERO else core)) * RD, 8), RD)
            def l_in(i, w): return pltpu.make_async_copy(HIDT.at[l, rows(i, w)], lhs.at[w], sems.at[w])
            def t_out(i): return pltpu.make_async_copy(tb, Td.at[mi, far(i)], sems.at[TWO])
            def m_out(i): return pltpu.make_async_copy(mb, OWNd.at[mi, far(i)], sems.at[3])
            l_in(ZERO, ZERO).start(); l_in(ZERO, ONE).start()
            def step(i, carry):
                l_in(i, ZERO).wait()
                @pl.when(i > ZERO)
                def _():
                    t_out(i - ONE).wait()
                    d0_copy(mi, i - ONE, far(i - ONE)).start()
                tb[...] = jnp.dot(lhs[ZERO], dyv[...], preferred_element_type=F32).astype(BF)
                t_out(i).start()
                @pl.when(i + ONE < chips)
                def _(): l_in(i + ONE, ZERO).start()
                l_in(i, ONE).wait()
                @pl.when(i > ZERO)
                def _(): m_out(i - ONE).wait()
                events(name, i, chips)
                mb[...] = jnp.dot(lhs[ONE], dyv[...], preferred_element_type=F32)
                m_out(i).start()
                @pl.when(i + ONE < chips)
                def _(): l_in(i + ONE, ONE).start()
                return carry
            lax.fori_loop(ZERO, chips, step, ZERO)
            t_out(chips - ONE).wait()
            d0_copy(mi, chips - ONE, far(chips - ONE)).start()
            m_out(chips - ONE).wait()
            for i in range(chips): sent.append(lambda i=i: d0_copy(mi, i, at_chip[FAR[i]]).wait_send())
        pl.run_scoped(body, pltpu.VMEM((TWO, RD, T), BF), pltpu.VMEM((RD, D), F32), pltpu.VMEM((RD, D), BF))

    def hidden_and_weights(name, l):
        gi, ui = GI[f"g{l}"], GI[f"u{l}"]
        def body(av, wbuf, gbuf, ubuf, dgbuf, dubuf, fg, fu, bg, bu):
            a_in = pltpu.make_async_copy(AT.at[l], av, sems.at[ZERO])
            a_in.start()
            def size(j): return rest if isinstance(j, int) and j == full else TN
            def at(j): return LAST if isinstance(j, int) and j == full else cols(j)
            def ins(j, s):
                w = pl.ds(ZERO, size(j))
                return [pltpu.make_async_copy(WD.at[l, at(j)], wbuf.at[s, w], sems.at[ONE + s]),
                        pltpu.make_async_copy(GATE.at[l, j, :, w], gbuf.at[s, :, w], sems.at[3 + s]),
                        pltpu.make_async_copy(UP.at[l, j, :, w], ubuf.at[s, :, w], sems.at[5 + s])]
            def states_out(j, s):
                if not l: return []
                w = pl.ds(ZERO, size(j))
                return [pltpu.make_async_copy(dgbuf.at[s, :, w], DG.at[:, at(j)], sems.at[7 + s]),
                        pltpu.make_async_copy(dubuf.at[s, :, w], DU.at[:, at(j)], sems.at[9 + s])]
            def terms_out(j):
                w = pl.ds(ZERO, size(j))
                return [pltpu.make_async_copy(fg.at[:, core, :, w], OWNg.at[gi, :, :, at(j)], sems.at[11]),
                        pltpu.make_async_copy(bg.at[:, ONE - core, :, w], Tg.at[gi, :, :, at(j)], sems.at[12]),
                        pltpu.make_async_copy(fu.at[:, core, :, w], OWNg.at[ui, :, :, at(j)], sems.at[13]),
                        pltpu.make_async_copy(bu.at[:, ONE - core, :, w], Tg.at[ui, :, :, at(j)], sems.at[14])]
            def first_half(j, s):
                w = pl.ds(ZERO, size(j))
                turned = wbuf[s, w].T
                for c in range(T // CH):
                    rows = pl.ds(c * CH, CH)
                    by = jnp.dot(dyv[rows], turned, preferred_element_type=F32).astype(BF).astype(F32)
                    g = gbuf[s, rows, w]
                    sig = ONE / (ONE + jnp.exp(-g))
                    silu = g * sig
                    dubuf[s, rows, w] = (by * silu).astype(BF)
                    dgbuf[s, rows, w] = (by * ubuf[s, rows, w] * (sig + silu * (ONE - sig))).astype(BF)
            def second_half(j, s):
                w = pl.ds(ZERO, size(j))
                for rhs, f, b in ((dgbuf, fg, bg), (dubuf, fu, bu)):
                    for c in range(chips):
                        got = jnp.dot(av[pl.ds(c * TWO * RG, TWO * RG)], rhs[s, :, w], preferred_element_type=F32)
                        for k in (ZERO, ONE):
                            f[c, k, :, w] = got[k * RG:(k + ONE) * RG]
                            b[c, k, :, w] = got[k * RG:(k + ONE) * RG].astype(BF)
            for c in ins(ZERO, ZERO): c.start()
            a_in.wait()
            def step(j, carry):
                s = lax.rem(j, TWO)
                for c in ins(j, s): c.wait()
                @pl.when(j + ONE < full)
                def _():
                    for c in ins(j + ONE, ONE - s): c.start()
                @pl.when(j + ONE == full)
                def _():
                    for c in ins(full, full % TWO): c.start()
                if l:
                    @pl.when(j >= TWO)
                    def _():
                        for c in states_out(j - TWO, s): c.wait()
                events(name, TWO * j, TWO * full, ZERO)
                first_half(j, s)
                for c in states_out(j, s): c.start()
                @pl.when(j >= ONE)
                def _():
                    for c in terms_out(j - ONE): c.wait()
                events(name, TWO * j + ONE, TWO * full, ONE)
                second_half(j, s)
                for c in terms_out(j): c.start()
                return carry
            lax.fori_loop(ZERO, full, step, ZERO)
            s = full % TWO
            for c in ins(full, s): c.wait()
            for c in states_out(full - TWO, s): c.wait()
            events_at(name, TWO * full)
            first_half(full, s)
            for c in states_out(full, s): c.start()
            for c in terms_out(full - ONE): c.wait()
            events_at(name, TWO * full + ONE)
            second_half(full, s)
            for c in terms_out(full): c.start()
            for c in states_out(full - ONE, ONE - s) + states_out(full, s) + terms_out(full): c.wait()
        V = pltpu.VMEM
        pl.run_scoped(body, V((D, T), BF), V((TWO, TN, D), BF), V((TWO, T, TN), F32), V((TWO, T, TN), F32), V((TWO, T, TN), BF), V((TWO, T, TN), BF),
                      V((chips, TWO, RG, TN), F32), V((chips, TWO, RG, TN), F32), V((chips, TWO, RG, TN), BF), V((chips, TWO, RG, TN), BF))

    def states(name, l):
        nd = D // TD
        def body(lg, lu, rg, ru, dav, hv):
            def ins(t, s):
                rows = pl.ds(pl.multiple_of(t * TB, TB), TB)
                return [pltpu.make_async_copy(DG.at[rows], lg.at[s], sems.at[s]), pltpu.make_async_copy(DU.at[rows], lu.at[s], sems.at[TWO + s])]
            def w_in(d, s):
                return [pltpu.make_async_copy(WGT.at[d], rg.at[s], sems.at[4 + s]), pltpu.make_async_copy(WUT.at[d], ru.at[s], sems.at[6 + s])]
            def h_in(t): return pltpu.make_async_copy(H1.at[pl.ds(pl.multiple_of(t * TB, TB), TB)], hv, sems.at[8])
            for c in ins(ZERO, ZERO) + w_in(ZERO, ZERO): c.start()
            def step(q, carry):
                t, d = lax.div(q, nd), lax.rem(q, nd)
                s, p = lax.rem(t, TWO), lax.rem(q, TWO)
                @pl.when(d == ZERO)
                def _():
                    for c in ins(t, s): c.wait()
                    h_in(t).start()
                    @pl.when(t + ONE < nt)
                    def _():
                        for c in ins(t + ONE, ONE - s): c.start()
                for c in w_in(d, p): c.wait()
                @pl.when(q + ONE < nt * nd)
                def _():
                    for c in w_in(lax.rem(q + ONE, nd), ONE - p): c.start()
                events(name, q, nt * nd)
                a = jnp.dot(lg[s], rg[p], preferred_element_type=F32).astype(BF)
                b = jnp.dot(lu[s], ru[p], preferred_element_type=F32).astype(BF)
                dav[:, pl.ds(pl.multiple_of(d * TD, TD), TD)] = (a.astype(F32) + b.astype(F32)).astype(BF)
                @pl.when(d == nd - ONE)
                def _():
                    h_in(t).wait()
                    def rows_of(i, carry):
                        rr = pl.ds(pl.multiple_of(i * 64, 64), 64)
                        wide, by = hv[rr].astype(F32), dav[rr].astype(F32)
                        scale = lax.rsqrt(jnp.mean(wide * wide, -ONE, keepdims=True) + 1e-6)
                        inner = jnp.sum(by * wide, -ONE, keepdims=True) * (scale * scale * scale / D)
                        back = (by * scale - wide * inner).astype(BF)
                        here = pl.ds(pl.multiple_of(t * TB + i * 64, 64), 64)
                        dyv[here] = (dyv[here].astype(F32) + back.astype(F32)).astype(BF)
                        return carry
                    lax.fori_loop(ZERO, TB // 64, rows_of, ZERO)
                return carry
            lax.fori_loop(ZERO, nt * nd, step, ZERO)
        V = pltpu.VMEM
        pl.run_scoped(body, V((TWO, TB, F), BF), V((TWO, TB, F), BF), V((TWO, F, TD), BF), V((TWO, F, TD), BF), V((TB, D), BF), V((TB, D), BF))

    down_weights("d1", ONE)
    hidden_and_weights("m1", ONE)
    states("a1", ONE)
    down_weights("d0", ZERO)
    hidden_and_weights("m0", ZERO)
    for e in tail: event(*e)
    for (kind, stage, k), q in user.items(): settle(q, stage)
    slots[me] = jnp.full(slots.shape[ONE:], jnp.sum(sqv[...]), F32)
    def total_copy(k, whose):
        return pltpu.make_async_remote_copy(src_ref=slots.at[whose], dst_ref=slots.at[whose], send_sem=ts.at[k], recv_sem=tr.at[whose],
                                            device_id=(r, others[k]), device_id_type=MESH)
    for k in range(n - ONE): total_copy(k, me).start()
    for c in sent: c()
    for k in range(n - ONE): total_copy(k, others[k]).wait_recv()
    for k in range(n - ONE): total_copy(k, me).wait_send()
    total = slots[ZERO]
    for k in range(ONE, n): total = total + slots[k]
    sqv[ZERO:8, ZERO:128] = total
    put = pltpu.make_async_copy(sqv.at[ZERO:8, ZERO:128], SQ, one)
    put.start()
    put.wait()


def bwd(n, dy, H1, WGT, WUT, WD, GATE, UP, HIDT, AT):
    T, D = dy.shape
    L, F, _ = WD.shape
    RG, RD, chips = D // n, F // n, n // TWO
    edges = [ZERO] + [k * TN for k in CUTS] + [F]
    wide_g, wide_d = max(b - a for a, b in zip(edges, edges[ONE:])), D // TWO
    nc = len(CUTS) + ONE
    S = jax.ShapeDtypeStruct
    A = pl.BlockSpec(memory_space=pl.ANY)
    DMA, V = pltpu.SemaphoreType.DMA, pltpu.VMEM
    ng, nd = TWO * L, L
    def adds(R, w, k): return [V((k, R, w), F32), V((k, R, w), BF), V((k, R, w), BF), V((k, R, w), BF)] + [V((k, R, w), BF)] * 4
    return pl.pallas_call(
        functools.partial(bwd_kernel, n),
        out_shape=[S((L, RG, F), BF), S((L, RG, F), BF), S((L, RD, D), BF), S((8, 128), F32), S((T, F), BF), S((T, F), BF),
                   S((ng, chips, RG, F), F32), S((ng, chips, RG, F), BF), S((ng, chips, RG, F), BF), S((ng, TWO, RG - RG // 32 * 16, F), BF), S((ng, TWO, RG, F), BF),
                   S((nd, chips, RD, D), F32), S((nd, chips, RD, D), BF), S((nd, chips, RD, D), BF), S((nd, TWO, RD - RD // 32 * 16, D), BF), S((nd, TWO, RD, D), BF)],
        in_specs=[A] * 9, out_specs=[A] * 16,
        scratch_shapes=[V((T, D), BF), V((8, max(wide_g, wide_d)), F32)] + adds(RG, wide_g, TWO) + adds(RD, wide_d, ONE) + [V((n, 8, 128), F32),
            DMA((4, nc)), DMA((4, nc)), DMA((TWO, 4)), DMA((TWO, 4)), DMA((6, nc, TWO)), DMA((6, nc, TWO)), DMA((6, nc, TWO)), DMA((6, nc, TWO)),
            DMA((12,)), DMA((3,)), DMA((16,)), DMA(()), DMA((n - ONE,)), DMA((n,))],
        compiler_params=pltpu.CompilerParams(collective_id=ONE, has_side_effects=True, vmem_limit_bytes=VMEM_LIMIT),
        name="backward",
    )(dy, H1, WGT, WUT, WD, GATE, UP, HIDT, AT)[:4]


def adamw(w, m, v, g):
    m = 0.9 * m + 0.1 * g
    v = 0.95 * v + 0.05 * g * g
    step = m * lax.rsqrt(v + 1e-8) + 0.1 * w
    return (w - 0.02 * step).astype(BF), m, v


def solution(mesh):
    n = mesh.shape["dp"]

    def step(x, dy, *arrays):
        weights, m, v = (arrays[i : i + 3] for i in (ZERO, 3, 6))
        _, _, WD, GATE, UP, HIDT, AT, H1, WGT, WUT = fwd(n, x[ZERO], *weights)
        *gradients, squares = bwd(n, dy[ZERO], H1, WGT, WUT, WD, GATE, UP, HIDT, AT)
        count = lax.psum(ONE, "dp") * sum(g.size for g in gradients)
        factor = jnp.minimum(1.0, 0.5 * lax.rsqrt(squares[ZERO, ZERO] / count + 1e-30))
        new = [adamw(w.astype(F32), m, v, g.astype(F32) * factor) for w, m, v, g in zip(weights, m, v, gradients, strict=True)]
        return tuple(one[which] for which in range(3) for one in new)

    states, cut = P(("rep", "dp"), None, None), P(None, "dp", None)
    return jax.shard_map(step, mesh=mesh, in_specs=(states, states) + (cut,) * 9, out_specs=(P("rep", "dp", None),) * 9, check_vma=False)
```

time: 1100 us -> 812 us (0.74)
  Pallas kernels: 0 us -> 765 us
  matrix products: 620 us -> 0 us
  waiting for transfers between devices: 349 us -> 0 us
  local copies, waits for them, and re-layouts: 30.9 us -> 2.36 us
  other arithmetic: 62.1 us -> 37.5 us
  between operations: 17.5 us -> 1.65 us
  blocking collectives: 13.3 us -> 0 us
    pallas_call x0 -> x2, Pallas kernels: none -> 765 us  [the longest x1 496 us: bwd(): pl.pallas_call(functools.partial(bwd_kernel, n), out_shape=[S((L, RG, F),...]
    dot_general x15 -> x0, matrix products: 620 us -> none  [the longest x5 217 us: layer(): up = jnp.dot(a, w['w_up'], preferred_element_type=jnp.float32)]
    reduce_scatter x6 -> x0, waiting for transfers between devices: 179 us -> none  [step(): lax.psum_scatter(by_w[name], 'dp', scatter_dimension=0, tiled=True)]
    all_gather x6 -> x0, waiting for transfers between devices: 167 us -> none  [fetched(): lax.all_gather(w[number], 'dp', axis=0, tiled=True)]
    unnamed x26 -> x6, local copies, waits for them, and re-layouts: 21.1 us -> 1.17 us
    reduce_sum x4 -> x0, other arithmetic: 16.8 us -> none  [the longest x3 12.7 us: step(): squares = lax.psum(sum((jnp.sum(g * g) for g in gradients)), 'dp')]
    psum x1 -> x0, blocking collectives: 13.3 us -> none  [step(): squares = lax.psum(sum((jnp.sum(g * g) for g in gradients)), 'dp')]
  transfers between devices with their start and end apart: 12 -> 0, of which waited for: 9 -> 0; matrix products, arithmetic and copies ran while one was open for 44% -> 0% of each run, Pallas kernels for 0% -> 0%
where the time goes in v2:
time: 812 us; the launch traced here: 807 us
  Pallas kernels  765 us (94%)
  other arithmetic  37.5 us (5%)
    pallas_call x1, Pallas kernels, bwd(): pl.pallas_call(functools.partial(bwd_kernel, n), out_shape=[S((L, RG, F),...  496 us
    pallas_call x1, Pallas kernels, fwd(): pl.pallas_call(functools.partial(fwd_kernel, n), out_shape=[S((L, D, F),...  269 us
    convert_element_type x2, other arithmetic, adamw(): return ((w - 0.02 * step).astype(BF), m, v)  37.5 us

profile of v2, /device:TPU:112, one launch (start us, length us, event | category | flops | bytes accessed | tf_op | source)
XLA Modules:
  0.0 806.9 jit_solution(13494360397615781184)
XLA Ops:
  0.6 269.3 %forward.1 = (bf16[2,1536,4224]{2,1,0:T(8,128)(2,1)}, bf16[2,1536,4224]{2,1,0:T(8,128)(2,1)}, bf16[2,4224,1536]{2,1,0:T(8,128)(2,1)}, f32[2,17,2048,256]{3,2,1,0...) custom-call(bf16[2048,1536]{1,0:T(8,128)(2,1)} %bitcast.3, ...), custom_call_target="tpu_custom_call" | custom-call | tf_op jit(solution)/shard_map/forward/pallas_call | solution.py:281
  269.9 496.2 %backward.1 = (bf16[2,192,4224]{2,1,0:T(8,128)(2,1)}, bf16[2,192,4224]{2,1,0:T(8,128)(2,1)}, bf16[2,528,1536]{2,1,0:T(8,128)(2,1)}, f32[8,128]{1,0:T(8,128)}, bf...) custom-call(bf16[2048,1536]{1,0:T(8,128)(2,1)} %bitcast.4, ...), custom_call_target="tpu_custom_call" | custom-call | tf_op jit(solution)/shard_map/backward/pallas_call | solution.py:769
  766.1 1.2 slice.3
  768.0 0.0 copy-start
  768.0 0.0 copy-start.1
  768.0 0.0 copy-start.2
  768.0 14.0 %fusion.8 = (bf16[2,528,1536]{2,1,0:T(8,128)(2,1)}, f32[2,528,1536]{2,1,0:T(8,128)}, f32[2,528,1536]{2,1,0:T(8,128)}) fusion(bf16[2,528,1536]{2,1,0:T(8,128)(2,1)} %wd.1, f32[]{:T(128)} %bitcast.2, bf16[2,528,1536]{2,1,0:T(8,128)(2,1)} %get-tuple-element.32, f32[2,528,1536]{2,1,0:T(8,128)} %param.21, f32[2,528,1536]{2,1,0:T(8,128)} %param.18), kind=kLoop, calls=%fused_computation.17 | loop fusion | flops 27574272 | bytes 35684356 | tf_op jit(solution)/shard_map/convert_element_type | solution.py:787
  782.0 0.0 copy-done
  782.0 0.0 copy-done.1
  782.0 1.2 copy-done.2
  783.2 23.5 %fusion.2 = (bf16[2,192,4224]{2,1,0:T(8,128)(2,1)}, f32[2,192,4224]{2,1,0:T(8,128)}, f32[2,192,4224]{2,1,0:T(8,128)}, bf16[2,192,4224]{2,1,0:T(8,128)(2,1)}, f32...) fusion(bf16[2,192,4224]{2,1,0:T(8,128)(2,1)S(1)} %copy-done, f32[]{:T(128)} %bitcast.2, ...), kind=kLoop, calls=%fused_computation.11 | loop fusion | flops 55148544 | bytes 71368704 | tf_op jit(solution)/shard_map/convert_element_type | solution.py:787
Async XLA Ops:
  768.0 14.0 %copy-start = (bf16[2,192,4224]{2,1,0:T(8,128)(2,1)S(1)}, bf16[2,192,4224]{2,1,0:T(8,128)(2,1)}, u32[]{:S(2)}) copy-start(bf16[2,192,4224]{2,1,0:T(8,128)(2,1)} %wg.1) | copy-start | bytes 9732100
  768.0 14.0 %copy-start.1 = (bf16[2,192,4224]{2,1,0:T(8,128)(2,1)S(1)}, bf16[2,192,4224]{2,1,0:T(8,128)(2,1)}, u32[]{:S(2)}) copy-start(bf16[2,192,4224]{2,1,0:T(8,128)(2,1)} %wu.1) | copy-start | bytes 9732100
  768.0 15.2 %copy-start.2 = (bf16[2,192,4224]{2,1,0:T(8,128)(2,1)S(1)}, bf16[2,192,4224]{2,1,0:T(8,128)(2,1)}, u32[]{:S(2)}) copy-start(bf16[2,192,4224]{2,1,0:T(8,128)(2,1)} %get-tuple-element.29) | copy-start | bytes 9732100
